TPU v7x, 1024 devices: a whole 4x8x16 slice. The times are simulated.
1024 devices in a mesh: gx: 16 (over y, core), gy: 16 (over z), gz: 4 (over x).
Axes of the slice: x: 4, y: 8, z: 16, core: 2. Of those that a mesh axis runs over, the one named last changes fastest.
Arguments:
- positions: float32 [3, 16, 16, 4, 512], P(None, 'gx', 'gy', 'gz'), may hold values from -6 to 6
- velocity: float32 [3, 16, 16, 4, 512], P(None, 'gx', 'gy', 'gz'), may hold values from -7.2 to 7.2
- atom_eps: float32 [16, 16, 4, 512], P('gx', 'gy', 'gz'), may hold values from 0.5 to 2
- neighbours: int32 [16, 16, 4, 32, 512], P('gx', 'gy', 'gz'), may hold values from 0 to 511
- pair_live: int32 [16, 16, 4, 32, 512], P('gx', 'gy', 'gz'), may hold values 0 or 1
- event_count: int32 [16, 16, 4], P('gx', 'gy', 'gz'), may hold values from 0 to 16, as said below
- event_atoms: int32 [16, 16, 4, 16, 128], P('gx', 'gy', 'gz'), may hold values from 0 to 2047
- event_weight: float32 [16, 16, 4, 16], P('gx', 'gy', 'gz'), may hold values from 0.2 to 1
- template_map: float32 [128, 128], replicated, may hold values from -0.5 to 0.5
Outputs:
- final_positions: float32 [3, 16, 16, 4, 512], P(None, 'gx', 'gy', 'gz')
- final_velocity: float32 [3, 16, 16, 4, 512], P(None, 'gx', 'gy', 'gz')
Inputs may be any that keep to these rules, and one draw needn't show every extreme that they name: `event_count`: in every column of domains along the third dimension, the counts add up to at most 32, and one domain of the column holds 16.
All inputs are finite; a program needn't handle non-finite values. No bound on the sum of `pair_live` on one device may be relied on, other than what follows from the above.
Results may differ from a plain program's by a relative error of at most 0.0003.
Values sent between devices are 32-bit elements; how exact they have to be, the bound alone decides.
No kernel may reach another device: no remote copies, remote signals or barrier semaphores. Data moves between devices by JAX's collectives and lax.ppermute only.
A program may use at most 64 MiB of HBM per device.

v0:
```python
import functools

import jax
import jax.numpy as jnp
from jax import lax
from jax.sharding import Mesh
from jax.sharding import PartitionSpec as P

EV_DEV = 16
NEIGH = 32
TEMPLATE = 128
FIRE_STEPS = 2
GX_GY_GZ = ("gx_0", "gx_1", "gy", "gz")
GX = ("gx_0", "gx_1")


width_scale = 1.5
time_step = 0.1
mixing = 0.1
epsilon = 1e-06


def laid_out(parts, dim):
    parts = jnp.moveaxis(parts, 0, dim)
    dims = parts.shape
    return parts.reshape(*dims[:dim], dims[dim] * dims[dim + 1], *dims[dim + 2 :])


def copy_for_each(x, axis):
    size = lax.axis_size(axis)
    return lax.all_to_all(jnp.broadcast_to(x[None], (size, *x.shape)), axis, 0, 0, tiled=True)


def gathered_copies(x, axis, dim):
    return laid_out(copy_for_each(x, axis), dim)


def cut_along(x, dim, size):
    before, after = (x.shape[:dim], x.shape[dim + 1 :])
    return jnp.moveaxis(x.reshape(*before, size, -1, *after), dim, 0)


def sent_and_summed(x, axis, dim):
    parts = cut_along(x, dim, lax.axis_size(axis))
    arrived = lax.all_to_all(parts, axis, split_axis=0, concat_axis=0, tiled=True)
    return arrived.sum(axis=0)


def with_halo(x, sides, width):
    for axis, dim in sides:
        size, length = (lax.axis_size(axis), x.shape[dim])
        up = [(i, (i + 1) % size) for i in range(size)]
        down = [(j, i) for i, j in up]
        last = lax.slice_in_dim(x, length - width, length, axis=dim)
        leading = lax.slice_in_dim(x, 0, width, axis=dim)
        before = lax.ppermute(last, axis, up)
        after = lax.ppermute(leading, axis, down)
        x = jnp.concatenate([before, x, after], axis=dim)
    return x


def over_axes(x, axes):
    return functools.reduce(lax.psum, axes, x)


def relax_events(group_positions, members, weights, template_map):
    gathered = jnp.take(group_positions, members, axis=1)
    centred = gathered - jnp.mean(gathered, axis=2, keepdims=True)
    shifted = jnp.einsum("cnt,ts->cns", centred, template_map, precision=lax.Precision.HIGHEST)
    shifted = shifted * weights[None, :, None]
    flattened = members.reshape(-1)
    return jnp.zeros_like(group_positions).at[:, flattened].add(shifted.reshape(3, -1))


def pair_forces(neighbourhood, own_atoms, neighbour_rows, live_pairs):
    partner = jnp.take(neighbourhood, neighbour_rows, axis=1)
    separation = own_atoms[:3, None, :] - partner[:3]
    distance_sq = jnp.sum(separation * separation, axis=0)
    strength = jnp.sqrt(own_atoms[3][None, :] * partner[3]) * live_pairs.astype(jnp.float32)
    strength = (
        strength
        * jnp.exp(-distance_sq * (0.5 / (width_scale * width_scale)))
        / (width_scale * width_scale)
    )
    return jnp.sum(strength[None] * separation, axis=1)


def shards(
    positions,
    velocity,
    atom_eps,
    neighbours,
    pair_live,
    event_count,
    event_atoms,
    event_weight,
    template_map,
):
    atom_count = positions.shape[4]
    group_size = lax.axis_size("gz")
    gathered = gathered_copies(positions, "gz", 3)
    group_positions = gathered.reshape(3, group_size * atom_count)
    alive_mask = jnp.arange(EV_DEV, dtype=jnp.int32) < event_count.reshape(())
    members = event_atoms.reshape(EV_DEV, TEMPLATE)
    weights = event_weight.reshape(EV_DEV) * alive_mask.astype(jnp.float32)
    displaced = relax_events(group_positions, members, weights, template_map).reshape(
        3, 1, 1, group_size, atom_count
    )
    returned = sent_and_summed(displaced, "gz", 3)
    moved_positions = positions + returned
    offsets = jnp.arange(NEIGH, dtype=jnp.int32) % 27 * atom_count
    neighbour_rows = neighbours.reshape(NEIGH, atom_count) + offsets[:, None]
    live_pairs = pair_live.reshape(NEIGH, atom_count)
    speeds = velocity
    for iteration in range(FIRE_STEPS):
        packed = jnp.concatenate([moved_positions, atom_eps[None]], 0)
        widened = with_halo(packed, ((GX, 1), ("gy", 2), ("gz", 3)), 1)
        neighbourhood = widened.reshape(4, 27 * atom_count)
        forces = pair_forces(
            neighbourhood, packed.reshape(4, atom_count), neighbour_rows, live_pairs
        ).reshape(moved_positions.shape)
        power_sum, speed_sq, force_sq = (
            over_axes(jnp.sum(forces * speeds), GX_GY_GZ),
            over_axes(jnp.sum(speeds * speeds), GX_GY_GZ),
            over_axes(jnp.sum(forces * forces), GX_GY_GZ),
        )
        cosine = power_sum / (jnp.sqrt(speed_sq + epsilon) * jnp.sqrt(force_sq + epsilon))
        speed_ratio = jnp.sqrt((speed_sq + epsilon) / (force_sq + epsilon))
        speeds = 0.5 * (1.0 + cosine) * ((1.0 - mixing) * speeds + mixing * speed_ratio * forces)
        speeds = speeds + time_step * forces
        moved_positions = moved_positions + time_step * speeds
    return (moved_positions, speeds)


def solution(mesh):
    split = Mesh(
        mesh.devices.reshape(8, 2, mesh.shape["gy"], mesh.shape["gz"]), ("gx_0", "gx_1", "gy", "gz")
    )
    in_specs = (
        P(None, GX, "gy", "gz", None),
        P(None, GX, "gy", "gz", None),
        P(GX, "gy", "gz", None),
        P(GX, "gy", "gz", None, None),
        P(GX, "gy", "gz", None, None),
        P(GX, "gy", "gz"),
        P(GX, "gy", "gz", None, None),
        P(GX, "gy", "gz", None),
        P(),
    )
    out_specs = (P(None, GX, "gy", "gz", None), P(None, GX, "gy", "gz", None))
    return jax.shard_map(
        shards, mesh=split, in_specs=in_specs, out_specs=out_specs, check_vma=False
    )
```

profile of v0, /device:TPU:8, one launch (start us, length us, event | category | flops | bytes accessed | tf_op | source)
XLA Modules:
  0.0 367.6 jit_solution(17460129770647011891)
XLA Ops:
  0.7 0.7 copy.78
  1.4 0.6 broadcast_in_dim.45
  2.0 4.3 %all-to-all-start = ((f32[4,3,1,1,1,512]{5,4,3,2,1,0:T(1,128)}), f32[4,3,1,1,1,512]{5,4,3,2,1,0:T(1,128)S(1)}, u32[]{:S(2)}, u32[]{:S(2)}) async-start(f32[4,3,1,1,1,512]{5,4,3,2,1,0:T(1,128)} %broadcast_in_dim.45), calls=%async_computation | async-start | bytes 49152 | tf_op jit(solution)/shard_map/all_to_all | solution.py:31
  6.3 0.7 fusion.51
  7.0 0.7 compare_and_fusion.1
  8.3 0.7 compare_select_fusion.1
  9.1 0.7 compare_select_fusion.4
  9.7 2.0 all-to-all-done
  11.7 0.4 copy.50
  12.1 5.5 %gather_fusion = f32[2048,3]{1,0:T(8,128)S(1)} fusion(f32[3,2048]{0,1:T(8,128)S(1)} %bitcast.110, s32[2048]{0:T(1024)S(1)} %fusion.51), kind=kCustom, calls=%fused_computation.2 | custom fusion | bytes 57344 | tf_op jit(solution)/shard_map/jit(_take)/gather | solution.py:67
  17.5 0.3 copy.51
  18.0 0.2 convolution_multiply_fusion
  18.2 0.4 copy.73
  18.6 11.7 %scatter_custom_fusion = f32[3,2048]{0,1:T(8,128)S(1)} fusion(s32[2048]{0:T(1024)S(1)} %bitcast.127, f32[2048,3]{1,0:T(8,128)S(1)} %bitcast.112, f32[]{:T(128)} %constant.20.clone.1), kind=kCustom, calls=%fused_computation.5 | custom fusion | flops 6144 | bytes 24580 | tf_op jit(solution)/shard_map/scatter-add | solution.py:72
  30.3 0.9 copy.53
  31.2 3.3 all-to-all-start.1
  34.5 0.9 fusion.41
  35.4 0.8 copy.55
  36.3 3.6 all-to-all-done.1
  39.9 0.1 copy.75
  40.2 0.7 pad_maximum_fusion.7
  40.9 1.7 collective-permute-start.1
  42.7 1.3 collective-permute-done
  44.0 0.7 fusion.43
  44.7 4.3 %collective-permute-start.2 = (f32[4,3,1,1,512]{4,0,3,2,1:T(4,128)S(1)}, f32[4,3,1,1,512]{4,0,3,2,1:T(4,128)S(1)}, u32[]{:S(2)}, u32[]{:S(2)}) collective-permute-start(f32[4,3,1,1,512]{4,0,3,2,1:T(4,128)S(1)} %fusion.43), channel_id=1, source_target_pairs={{0,4},{4,8},{8,12},{12,16},{16,20},{20,24},{24,28},{28,32},{32,36}... | collective-permute-start | bytes 73736 | tf_op jit(solution)/shard_map/ppermute | solution.py:56
  49.0 15.9 %collective-permute-start.3 = (f32[4,3,1,1,512]{4,0,3,2,1:T(4,128)S(1)}, f32[4,3,1,1,512]{4,0,3,2,1:T(4,128)S(1)}, u32[]{:S(2)}, u32[]{:S(2)}) collective-permute-start(f32[4,3,1,1,512]{4,0,3,2,1:T(4,128)S(1)} %fusion.43), channel_id=1, source_target_pairs={{4,0},{8,4},{12,8},{16,12},{20,16},{24,20},{28,24},{32,28},{36,32}... | collective-permute-start | bytes 73736 | tf_op jit(solution)/shard_map/ppermute | solution.py:57
  64.9 0.9 compare_and_fusion
  65.8 0.6 collective-permute-done.3
  66.4 0.7 fusion.25
  67.1 2.5 collective-permute-start.4
  69.6 4.6 %collective-permute-start.5 = (f32[4,3,3,1,512]{4,0,3,2,1:T(4,128)S(1)}, f32[4,3,3,1,512]{4,0,3,2,1:T(4,128)S(1)}, u32[]{:S(2)}, u32[]{:S(2)}) collective-permute-start(f32[4,3,3,1,512]{4,0,3,2,1:T(4,128)S(1)} %fusion.25), channel_id=1, source_target_pairs={{1,0},{2,1},{3,2},{0,3},{5,4},{6,5},{7,6},{4,7},{9,8},{10,9},{11,1... | collective-permute-start | bytes 221192 | tf_op jit(solution)/shard_map/ppermute | solution.py:57
  74.2 1.3 multiply_reduce_fusion.7
  75.5 0.8 copy.62
  76.3 0.1 copy.64
  76.7 4.3 %copy.58 = f32[4,3,3,3,512]{0,4,3,2,1:T(8,128)} copy(f32[4,3,3,3,512]{4,0,3,2,1:T(4,128)S(1)} %fusion.15) | data formatting | bytes 442368 | tf_op jit(solution)/shard_map/concatenate | solution.py:58
  81.0 57.4 %gather_fusion.1 = f32[16384,4]{1,0:T(8,128)} fusion(f32[4,13824]{0,1:T(8,128)} %bitcast.104, s32[16384]{0:T(1024)S(1)} %broadcast_clamp_fusion), kind=kCustom, calls=%fused_computation.clone | custom fusion | bytes 589824 | tf_op jit(solution)/shard_map/jit(_take)/gather | solution.py:76
  138.4 5.2 %copy.59 = f32[32,512,4]{1,0,2:T(8,128)S(1)} copy(f32[32,512,4]{2,1,0:T(8,128)} %bitcast.106) | data formatting | bytes 524288 | tf_op jit(solution)/shard_map/jit(_take)/gather | solution.py:76
  143.8 0.1 copy.61
  144.0 0.6 multiply_reduce_fusion.6
  144.6 0.7 fusion.6
  145.2 17.5 %all-reduce.3 = (f32[]{:T(128)}, f32[]{:T(128)}, f32[]{:T(128)}) all-reduce(f32[]{:T(128)} %get-tuple-element.39, f32[]{:T(128)} %multiply_reduce_fusion.6, f32[]{:T(128)} %fusion.6), channel_id=1, replica_groups=mesh['gx_0'=8,'gx_1'=2,'gy'=16,'gz'=4] {'gx_0'}, use_global_device_ids=true, to_apply=%region_11.13 | all-reduce | flops 3 | bytes 24 | tf_op jit(solution)/shard_map/psum | solution.py:63
  162.7 3.2 all-reduce.7
  165.9 31.1 %all-reduce.1 = (f32[]{:T(128)}, f32[]{:T(128)}, f32[]{:T(128)}) all-reduce(f32[]{:T(128)} %get-tuple-element.32, f32[]{:T(128)} %get-tuple-element.33, f32[]{:T(128)} %get-tuple-element.34), channel_id=1, replica_groups=mesh['gx_0'=8,'gx_1'=2,'gy'=16,'gz'=4] {'gy'}, use_global_device_ids=true, to_apply=%region_13.15 | all-reduce | flops 3 | bytes 24 | tf_op jit(solution)/shard_map/psum | solution.py:63
  197.0 11.5 %all-reduce.5 = (f32[]{:T(128)}, f32[]{:T(128)}, f32[]{:T(128)}) all-reduce(f32[]{:T(128)} %get-tuple-element.14, f32[]{:T(128)} %get-tuple-element.15, f32[]{:T(128)} %get-tuple-element.16), channel_id=1, replica_groups=mesh['gx_0'=8,'gx_1'=2,'gy'=16,'gz'=4] {'gz'}, use_global_device_ids=true, to_apply=%region_14.16 | all-reduce | flops 3 | bytes 24 | tf_op jit(solution)/shard_map/psum | solution.py:63
  210.9 1.7 collective-permute-start.7
  212.7 1.3 collective-permute-done.6
  214.1 1.9 collective-permute-start.8
  216.0 5.1 %collective-permute-start.9 = (f32[4,3,1,1,512]{4,0,3,2,1:T(4,128)S(1)}, f32[4,3,1,1,512]{4,0,3,2,1:T(4,128)S(1)}, u32[]{:S(2)}, u32[]{:S(2)}) collective-permute-start(f32[4,3,1,1,512]{4,0,3,2,1:T(4,128)S(1)} %fusion.45), channel_id=1, source_target_pairs={{4,0},{8,4},{12,8},{16,12},{20,16},{24,20},{28,24},{32,28},{36,32}... | collective-permute-start | bytes 73736 | tf_op jit(solution)/shard_map/ppermute | solution.py:57
  221.2 1.4 collective-permute-done.9
  222.6 1.9 collective-permute-start.10
  224.6 5.1 %collective-permute-start.11 = (f32[4,3,3,1,512]{4,0,3,2,1:T(4,128)S(1)}, f32[4,3,3,1,512]{4,0,3,2,1:T(4,128)S(1)}, u32[]{:S(2)}, u32[]{:S(2)}) collective-permute-start(f32[4,3,3,1,512]{4,0,3,2,1:T(4,128)S(1)} %fusion.29), channel_id=1, source_target_pairs={{1,0},{2,1},{3,2},{0,3},{5,4},{6,5},{7,6},{4,7},{9,8},{10,9},{11,1... | collective-permute-start | bytes 221192 | tf_op jit(solution)/shard_map/ppermute | solution.py:57
  229.8 0.3 collective-permute-done.10
  230.1 1.6 collective-permute-done.11
  231.7 4.3 %copy.67 = f32[4,3,3,3,512]{0,4,3,2,1:T(8,128)} copy(f32[4,3,3,3,512]{4,0,3,2,1:T(4,128)S(1)} %fusion.21) | data formatting | bytes 442368 | tf_op jit(solution)/shard_map/concatenate | solution.py:58
  236.0 57.4 %gather_fusion.2 = f32[16384,4]{1,0:T(8,128)} fusion(f32[4,13824]{0,1:T(8,128)} %bitcast.103, s32[16384]{0:T(1024)S(1)} %broadcast_clamp_fusion), kind=kCustom, calls=%fused_computation.1.clone | custom fusion | bytes 589824 | tf_op jit(solution)/shard_map/jit(_take)/gather | solution.py:76
  293.5 5.2 %copy.68 = f32[32,512,4]{1,0,2:T(8,128)S(1)} copy(f32[32,512,4]{2,1,0:T(8,128)} %bitcast.105) | data formatting | bytes 524288 | tf_op jit(solution)/shard_map/jit(_take)/gather | solution.py:76
  299.0 0.6 multiply_reduce_fusion.5
  299.6 0.7 fusion.2
  300.3 17.4 %all-reduce.2 = (f32[]{:T(128)}, f32[]{:T(128)}, f32[]{:T(128)}) all-reduce(f32[]{:T(128)} %get-tuple-element.10, f32[]{:T(128)} %multiply_reduce_fusion.5, f32[]{:T(128)} %get-tuple-element.9), channel_id=1, replica_groups=mesh['gx_0'=8,'gx_1'=2,'gy'=16,'gz'=4] {'gx_0'}, use_global_device_ids=true, to_apply=%region_28.30 | all-reduce | flops 3 | bytes 24 | tf_op jit(solution)/shard_map/psum | solution.py:63
  317.7 3.2 all-reduce.6
  320.8 31.1 %all-reduce = (f32[]{:T(128)}, f32[]{:T(128)}, f32[]{:T(128)}) all-reduce(f32[]{:T(128)} %get-tuple-element.29, f32[]{:T(128)} %get-tuple-element.30, f32[]{:T(128)} %get-tuple-element.31), channel_id=1, replica_groups=mesh['gx_0'=8,'gx_1'=2,'gy'=16,'gz'=4] {'gy'}, use_global_device_ids=true, to_apply=%region_30.32 | all-reduce | flops 3 | bytes 24 | tf_op jit(solution)/shard_map/psum | solution.py:63
  352.0 12.0 %all-reduce.4 = (f32[]{:T(128)}, f32[]{:T(128)}, f32[]{:T(128)}) all-reduce(f32[]{:T(128)} %get-tuple-element.11, f32[]{:T(128)} %get-tuple-element.12, f32[]{:T(128)} %get-tuple-element.13), channel_id=1, replica_groups=mesh['gx_0'=8,'gx_1'=2,'gy'=16,'gz'=4] {'gz'}, use_global_device_ids=true, to_apply=%region_31.33 | all-reduce | flops 3 | bytes 24 | tf_op jit(solution)/shard_map/psum | solution.py:63
  366.2 0.7 copy.71
  366.9 0.7 copy.72
  (41 shorter events, 1.6 us)
Async XLA Ops:
  0.6 17.3 %copy-start = (f32[128,128]{1,0:T(8,128)S(1)}, f32[128,128]{1,0:T(8,128)}, u32[]{:S(2)}) copy-start(f32[128,128]{1,0:T(8,128)} %param.19) | copy-start | bytes 196612
  0.6 75.9 %copy-start.2 = (f32[1,1,1,512]{3,2,1,0:T(1,128)S(1)}, f32[1,1,1,512]{3,2,1,0:T(1,128)}, u32[]{:S(2)}) copy-start(f32[1,1,1,512]{3,2,1,0:T(1,128)} %param.13) | copy-start | bytes 6148
  2.0 9.7 %all-to-all-start = ((f32[4,3,1,1,1,512]{5,4,3,2,1,0:T(1,128)}), f32[4,3,1,1,1,512]{5,4,3,2,1,0:T(1,128)S(1)}, u32[]{:S(2)}, u32[]{:S(2)}) async-start(f32[4,3,1,1,1,512]{5,4,3,2,1,0:T(1,128)} %broadcast_in_dim.45), calls=%async_computation | async-start | bytes 49152 | tf_op jit(solution)/shard_map/all_to_all | solution.py:31
  31.2 8.6 %all-to-all-start.1 = ((f32[4,3,1,1,1,512]{5,4,3,2,1,0:T(1,128)}), f32[4,3,1,1,1,512]{5,4,3,2,1,0:T(1,128)S(1)}, u32[]{:S(2)}, u32[]{:S(2)}) async-start(f32[4,3,1,1,1,512]{5,4,3,2,1,0:T(1,128)} %bitcast.15), calls=%async_computation.1 | async-start | bytes 49152 | tf_op jit(solution)/shard_map/all_to_all | solution.py:45
  40.9 3.1 collective-permute-start
  40.9 3.1 collective-permute-start.1
  44.7 21.1 %collective-permute-start.2 = (f32[4,3,1,1,512]{4,0,3,2,1:T(4,128)S(1)}, f32[4,3,1,1,512]{4,0,3,2,1:T(4,128)S(1)}, u32[]{:S(2)}, u32[]{:S(2)}) collective-permute-start(f32[4,3,1,1,512]{4,0,3,2,1:T(4,128)S(1)} %fusion.43), channel_id=1, source_target_pairs={{0,4},{4,8},{8,12},{12,16},{16,20},{20,24},{24,28},{28,32},{32,36}... | collective-permute-start | bytes 73736 | tf_op jit(solution)/shard_map/ppermute | solution.py:56
  49.0 17.4 %collective-permute-start.3 = (f32[4,3,1,1,512]{4,0,3,2,1:T(4,128)S(1)}, f32[4,3,1,1,512]{4,0,3,2,1:T(4,128)S(1)}, u32[]{:S(2)}, u32[]{:S(2)}) collective-permute-start(f32[4,3,1,1,512]{4,0,3,2,1:T(4,128)S(1)} %fusion.43), channel_id=1, source_target_pairs={{4,0},{8,4},{12,8},{16,12},{20,16},{24,20},{28,24},{32,28},{36,32}... | collective-permute-start | bytes 73736 | tf_op jit(solution)/shard_map/ppermute | solution.py:57
  67.1 9.5 %collective-permute-start.4 = (f32[4,3,3,1,512]{4,0,3,2,1:T(4,128)S(1)}, f32[4,3,3,1,512]{4,0,3,2,1:T(4,128)S(1)}, u32[]{:S(2)}, u32[]{:S(2)}) collective-permute-start(f32[4,3,3,1,512]{4,0,3,2,1:T(4,128)S(1)} %fusion.25), channel_id=1, source_target_pairs={{0,1},{1,2},{2,3},{3,0},{4,5},{5,6},{6,7},{7,4},{8,9},{9,10},{10,1... | collective-permute-start | bytes 221192 | tf_op jit(solution)/shard_map/ppermute | solution.py:56
  69.6 7.0 %collective-permute-start.5 = (f32[4,3,3,1,512]{4,0,3,2,1:T(4,128)S(1)}, f32[4,3,3,1,512]{4,0,3,2,1:T(4,128)S(1)}, u32[]{:S(2)}, u32[]{:S(2)}) collective-permute-start(f32[4,3,3,1,512]{4,0,3,2,1:T(4,128)S(1)} %fusion.25), channel_id=1, source_target_pairs={{1,0},{2,1},{3,2},{0,3},{5,4},{6,5},{7,6},{4,7},{9,8},{10,9},{11,1... | collective-permute-start | bytes 221192 | tf_op jit(solution)/shard_map/ppermute | solution.py:57
  76.7 67.0 %copy-start.1 = (s32[1,1,1,32,512]{4,3,2,1,0:T(8,128)S(1)}, s32[1,1,1,32,512]{4,3,2,1,0:T(8,128)}, u32[]{:S(2)}) copy-start(s32[1,1,1,32,512]{4,3,2,1,0:T(8,128)} %param.15) | copy-start | bytes 196612
  210.9 3.1 collective-permute-start.6
  210.9 3.1 collective-permute-start.7
  214.1 7.1 %collective-permute-start.8 = (f32[4,3,1,1,512]{4,0,3,2,1:T(4,128)S(1)}, f32[4,3,1,1,512]{4,0,3,2,1:T(4,128)S(1)}, u32[]{:S(2)}, u32[]{:S(2)}) collective-permute-start(f32[4,3,1,1,512]{4,0,3,2,1:T(4,128)S(1)} %fusion.45), channel_id=1, source_target_pairs={{0,4},{4,8},{8,12},{12,16},{16,20},{20,24},{24,28},{28,32},{32,36}... | collective-permute-start | bytes 73736 | tf_op jit(solution)/shard_map/ppermute | solution.py:56
  216.0 6.6 %collective-permute-start.9 = (f32[4,3,1,1,512]{4,0,3,2,1:T(4,128)S(1)}, f32[4,3,1,1,512]{4,0,3,2,1:T(4,128)S(1)}, u32[]{:S(2)}, u32[]{:S(2)}) collective-permute-start(f32[4,3,1,1,512]{4,0,3,2,1:T(4,128)S(1)} %fusion.45), channel_id=1, source_target_pairs={{4,0},{8,4},{12,8},{16,12},{20,16},{24,20},{28,24},{32,28},{36,32}... | collective-permute-start | bytes 73736 | tf_op jit(solution)/shard_map/ppermute | solution.py:57
  222.6 7.5 %collective-permute-start.10 = (f32[4,3,3,1,512]{4,0,3,2,1:T(4,128)S(1)}, f32[4,3,3,1,512]{4,0,3,2,1:T(4,128)S(1)}, u32[]{:S(2)}, u32[]{:S(2)}) collective-permute-start(f32[4,3,3,1,512]{4,0,3,2,1:T(4,128)S(1)} %fusion.29), channel_id=1, source_target_pairs={{0,1},{1,2},{2,3},{3,0},{4,5},{5,6},{6,7},{7,4},{8,9},{9,10},{10,1... | collective-permute-start | bytes 221192 | tf_op jit(solution)/shard_map/ppermute | solution.py:56
  224.6 7.1 %collective-permute-start.11 = (f32[4,3,3,1,512]{4,0,3,2,1:T(4,128)S(1)}, f32[4,3,3,1,512]{4,0,3,2,1:T(4,128)S(1)}, u32[]{:S(2)}, u32[]{:S(2)}) collective-permute-start(f32[4,3,3,1,512]{4,0,3,2,1:T(4,128)S(1)} %fusion.29), channel_id=1, source_target_pairs={{1,0},{2,1},{3,2},{0,3},{5,4},{6,5},{7,6},{4,7},{9,8},{10,9},{11,1... | collective-permute-start | bytes 221192 | tf_op jit(solution)/shard_map/ppermute | solution.py:57
where the time goes:
time: 369 us; the launch traced here: 368 us
  local copies, waits for them, and re-layouts  147 us (40%)
  blocking collectives  127 us (34%)
  starting transfers between devices  52.3 us (14%)
  other arithmetic  23.1 us (6%)
  waiting for transfers between devices  12.2 us (3%)
  between operations  5.98 us (2%)
    psum x8, blocking collectives, over_axes(): return functools.reduce(lax.psum, axes, x)  127 us
    gather x4, local copies, waits for them, and re-layouts, pair_forces(): partner = jnp.take(neighbourhood, neighbour_rows, axis=1)  125 us
    ppermute x6, starting transfers between devices, with_halo(): after = lax.ppermute(leading, axis, down)  34.2 us
    scatter-add x1, other arithmetic, relax_events(): jnp.zeros_like(group_positions).at[:, flattened].add(shifted.reshape(3, -1))  11.7 us
    ppermute x6, starting transfers between devices, with_halo(): before = lax.ppermute(last, axis, up)  10.6 us
    concatenate x2, local copies, waits for them, and re-layouts, with_halo(): x = jnp.concatenate([before, x, after], axis=dim)  8.61 us
  transfers between devices with their start and end apart: 14, of which 9 were waited for; matrix products, arithmetic and copies ran while one was open for 2% of the time, Pallas kernels for 0%

commit v1 on v0

v1 whole, which is shorter than its diff:
```python
import jax
import jax.numpy as jnp
from jax import lax
from jax.experimental import pallas as pl
from jax.experimental.pallas import tpu as pltpu
from jax.sharding import Mesh
from jax.sharding import PartitionSpec as P

EV_DEV = 16
NEIGH = 32
TEMPLATE = 128
GX = ("gx_0", "gx_1")
GXZ = ("gx_0", "gx_1", "gz")
COLUMN = 4
CHUNKS = 4
LANES = 128
F32 = jnp.float32

width_scale = 1.5
time_step = 0.1
mixing = 0.1
epsilon = 1e-06

SMEM = pl.BlockSpec(memory_space=pltpu.SMEM)
VMEM = pl.BlockSpec(memory_space=pltpu.VMEM)


def call(kernel, outs, specs, scratch=(), flops=10000):
    return pl.pallas_call(
        kernel,
        out_shape=[jax.ShapeDtypeStruct(shape, F32) for shape in outs],
        in_specs=specs,
        out_specs=[VMEM] * len(outs),
        scratch_shapes=list(scratch),
        cost_estimate=pl.CostEstimate(flops=flops, bytes_accessed=100000, transcendentals=0),
    )


def pack_kernel(count_ref, pos_ref, vel_ref, eps_ref, weight_ref, atoms_ref, out_ref):
    live = lax.broadcasted_iota(jnp.int32, (1, EV_DEV), 1) < count_ref[0, 0, 0]
    weights = jnp.where(live, weight_ref[0, 0, :, :], 0.0)
    atoms = atoms_ref[0, 0, 0, :, :].astype(F32)
    for copy in range(COLUMN):
        out_ref[copy, 24:32, :] = jnp.zeros((8, LANES), F32)
        for c in range(3):
            for q in range(CHUNKS):
                cut = pl.ds(q * LANES, LANES)
                out_ref[copy, c * 4 + q : c * 4 + q + 1, :] = pos_ref[c, 0, 0, :, cut]
                out_ref[copy, 16 + c * 4 + q : 17 + c * 4 + q, :] = vel_ref[c, 0, 0, :, cut]
        for q in range(CHUNKS):
            out_ref[copy, 12 + q : 13 + q, :] = eps_ref[0, 0, :, pl.ds(q * LANES, LANES)]
        out_ref[copy, 28:29, 0:EV_DEV] = weights
        out_ref[copy, 32:48, :] = atoms


def events_kernel(column_ref, map_ref, moved_ref, vel_ref, low_ref, high_ref, shift_ref):
    slots = COLUMN * EV_DEV
    atoms = jnp.concatenate([column_ref[z, 32:48, :] for z in range(COLUMN)], 0).astype(jnp.int32)
    low, high = atoms & (LANES - 1), atoms >> 7
    low_ref[...] = low
    high_ref[...] = high
    diagonal = lax.broadcasted_iota(jnp.int32, (EV_DEV, LANES), 0) == lax.broadcasted_iota(
        jnp.int32, (EV_DEV, LANES), 1
    )
    weights = jnp.concatenate(
        [
            jnp.sum(jnp.where(diagonal, column_ref[z, 28:29, :], 0.0), axis=1, keepdims=True)
            for z in range(COLUMN)
        ],
        0,
    )
    centred = []
    for c in range(3):
        taken = jnp.zeros((slots, LANES), F32)
        for h in range(COLUMN * CHUNKS):
            z, q = divmod(h, CHUNKS)
            row = jnp.broadcast_to(column_ref[z, c * 4 + q : c * 4 + q + 1, :], (slots, LANES))
            taken = jnp.where(high == h, jnp.take_along_axis(row, low, axis=1), taken)
        centred.append(taken - jnp.sum(taken, axis=1, keepdims=True) * (1.0 / TEMPLATE))
    shift = jnp.dot(
        jnp.concatenate(centred, 0),
        map_ref[...],
        precision=lax.Precision.HIGHEST,
        preferred_element_type=F32,
    )
    shift = shift * jnp.concatenate([weights] * 3, 0)
    for part in range(3):
        rounded = shift.astype(jnp.bfloat16).astype(F32)
        for c in range(3):
            shift_ref[part * 3 + c, :, :] = rounded[c * slots : (c + 1) * slots]
        shift = shift - rounded
    places = lax.broadcasted_iota(jnp.int32, (LANES, LANES), 0)
    rows = lax.broadcasted_iota(jnp.int32, (16, LANES), 0)

    def some_events(i, total):
        lefts, rights = [], []
        for j in range(4):
            e = pl.ds(i * 4 + j, 1)
            here = high_ref[e, :] == rows
            left = [jnp.where(here, shift_ref[n, e, :], 0.0) for n in range(9)]
            lefts.append(jnp.concatenate(left, 0).astype(jnp.bfloat16))
            rights.append(jnp.where(low_ref[e, :] == places, 1.0, 0.0).astype(jnp.bfloat16))
        return total + lax.dot_general(
            jnp.concatenate(lefts, 1),
            jnp.concatenate(rights, 1),
            (((1,), (1,)), ((), ())),
            preferred_element_type=F32,
        )

    total = lax.fori_loop(0, slots // 4, some_events, jnp.zeros((144, LANES), F32))
    displaced = total[0:48] + total[48:96] + total[96:144]
    for z in range(COLUMN):
        for c in range(3):
            there = pl.ds(c * 16 + z * 4, 4)
            moved_ref[there, :] = (
                column_ref[z, c * 4 : c * 4 + 4, :] + displaced[c * 16 + z * 4 : c * 16 + z * 4 + 4]
            )
            vel_ref[there, :] = column_ref[z, 16 + c * 4 : 20 + c * 4, :]
        moved_ref[pl.ds(48 + z * 4, 4), :] = column_ref[z, 12:16, :]


def own_forces(z, source, neigh_ref, live_ref, table_ref):
    for k in range(NEIGH):
        ab, dz = divmod(k % 27, 3)
        a, b = divmod(ab, 3)
        first = ((z + dz + 3) & 3) * 4
        for c in range(4):
            for q in range(CHUNKS):
                table_ref[c, q, k : k + 1, :] = source(a, b, c, first + q)
    forces = [[None] * CHUNKS for _ in range(3)]
    for t in range(CHUNKS):
        own = [source(1, 1, c, z * 4 + t) for c in range(4)]
        total = [jnp.zeros((8, LANES), F32)] * 3
        for g in range(NEIGH // 8):
            atoms = neigh_ref[0, 0, 0, 8 * g : 8 * g + 8, t * LANES : (t + 1) * LANES]
            live = live_ref[0, 0, 0, 8 * g : 8 * g + 8, t * LANES : (t + 1) * LANES].astype(F32)
            low, high = atoms & (LANES - 1), atoms >> 7
            taken = []
            for c in range(4):
                value = jnp.take_along_axis(table_ref[c, 0, 8 * g : 8 * g + 8, :], low, axis=1)
                for q in range(1, CHUNKS):
                    other = jnp.take_along_axis(table_ref[c, q, 8 * g : 8 * g + 8, :], low, axis=1)
                    value = jnp.where(high == q, other, value)
                taken.append(value)
            apart = [own[c] - taken[c] for c in range(3)]
            square = apart[0] * apart[0] + apart[1] * apart[1] + apart[2] * apart[2]
            strength = jnp.sqrt(own[3] * taken[3]) * live
            strength = (
                strength
                * jnp.exp(-square * (0.5 / (width_scale * width_scale)))
                * (1.0 / (width_scale * width_scale))
            )
            total = [total[c] + strength * apart[c] for c in range(3)]
        for c in range(3):
            forces[c][t] = jnp.sum(total[c], axis=0, keepdims=True)
    return forces


def three_sums(forces, speeds):
    pairs = ((forces, speeds), (speeds, speeds), (forces, forces))
    lane = lax.broadcasted_iota(jnp.int32, (1, LANES), 1)
    packed = jnp.zeros((1, LANES), F32)
    for n, (left, right) in enumerate(pairs):
        added = sum(left[c][t] * right[c][t] for c in range(3) for t in range(CHUNKS))
        packed = jnp.where(lane == n, jnp.sum(added, axis=1, keepdims=True), packed)
    return packed


def read_sums(summed):
    lane = lax.broadcasted_iota(jnp.int32, (1, LANES), 1)
    return [
        jnp.sum(jnp.where(lane == n, summed, 0.0), axis=1, keepdims=True) for n in range(3)
    ]


def mix_factors(sums):
    power_sum, speed_sq, force_sq = sums
    cosine = power_sum / (jnp.sqrt(speed_sq + epsilon) * jnp.sqrt(force_sq + epsilon))
    speed_ratio = jnp.sqrt((speed_sq + epsilon) / (force_sq + epsilon))
    return 0.5 * (1.0 + cosine), mixing * speed_ratio


def new_speed(factors, speed, force):
    scale, ratio = factors
    return scale * ((1.0 - mixing) * speed + ratio * force) + time_step * force


def first_kernel(z_ref, m_ref, o_ref, p_ref, vel_ref, neigh_ref, live_ref, out_ref, table_ref):
    z = z_ref[0]
    halo = (m_ref, o_ref, p_ref)
    source = lambda a, b, c, row: halo[a][b, pl.ds(c * 16 + row, 1), :]
    forces = own_forces(z, source, neigh_ref, live_ref, table_ref)
    speeds = [
        [vel_ref[pl.ds(c * 16 + z * 4 + t, 1), :] for t in range(CHUNKS)] for c in range(3)
    ]
    sums = three_sums(forces, speeds)
    for copy in range(COLUMN):
        for c in range(3):
            for t in range(CHUNKS):
                out_ref[copy, c * 4 + t : c * 4 + t + 1, :] = forces[c][t]
        out_ref[copy, 12:16, :] = jnp.broadcast_to(sums, (4, LANES))


def column_kernel(parts_ref, vel_ref, out_ref, sums_ref):
    for z in range(COLUMN):
        for c in range(3):
            out_ref[pl.ds(c * 16 + z * 4, 4), :] = parts_ref[z, c * 4 : c * 4 + 4, :]
    out_ref[48:96, :] = vel_ref[...]
    total = sum(parts_ref[z, 12:13, :] for z in range(COLUMN))
    for n in range(sums_ref.shape[0]):
        sums_ref[n, :, :] = total


def second_kernel(
    z_ref, m_ref, o_ref, p_ref, fm_ref, fo_ref, fp_ref, sums_ref, neigh_ref, live_ref,
    out_ref, own_sums_ref, table_ref, new_ref,
):
    z = z_ref[0]
    factors = mix_factors(read_sums(jnp.sum(sums_ref[...], axis=0)))
    halo, pushed = (m_ref, o_ref, p_ref), (fm_ref, fo_ref, fp_ref)
    for a in range(3):
        for b in range(3):
            speed = new_speed(factors, pushed[a][b, 48:96, :], pushed[a][b, 0:48, :])
            new_ref[a * 3 + b, 0:48, :] = halo[a][b, 0:48, :] + time_step * speed
            new_ref[a * 3 + b, 48:64, :] = halo[a][b, 48:64, :]
            if a == 1 and b == 1:
                new_ref[9, 0:48, :] = speed
    source = lambda a, b, c, row: new_ref[a * 3 + b, pl.ds(c * 16 + row, 1), :]
    forces = own_forces(z, source, neigh_ref, live_ref, table_ref)
    own = lambda n: [
        [new_ref[n, pl.ds(c * 16 + z * 4 + t, 1), :] for t in range(CHUNKS)] for c in range(3)
    ]
    places, speeds = own(4), own(9)
    for c in range(3):
        for t in range(CHUNKS):
            out_ref[c * 4 + t : c * 4 + t + 1, :] = places[c][t]
            out_ref[12 + c * 4 + t : 13 + c * 4 + t, :] = speeds[c][t]
            out_ref[24 + c * 4 + t : 25 + c * 4 + t, :] = forces[c][t]
    sums = three_sums(forces, speeds)
    for n in range(own_sums_ref.shape[0]):
        own_sums_ref[n, :, :] = sums


def final_kernel(own_ref, sums_ref, pos_ref, vel_ref):
    factors = mix_factors(read_sums(jnp.sum(sums_ref[...], axis=0)))
    speed = new_speed(factors, own_ref[12:24, :], own_ref[24:36, :])
    place = own_ref[0:12, :] + time_step * speed
    for c in range(3):
        for t in range(CHUNKS):
            cut = pl.ds(t * LANES, LANES)
            pos_ref[c, 0, 0, :, cut] = place[c * 4 + t : c * 4 + t + 1]
            vel_ref[c, 0, 0, :, cut] = speed[c * 4 + t : c * 4 + t + 1]


def exchanged(x, axes):
    return lax.all_to_all(x, axes, 0, 0, tiled=True)


def added_for_each(parts, count):
    return jnp.broadcast_to(jnp.sum(parts, 0, keepdims=True), (count, 1, LANES))


def both_sides(x, axis):
    size = lax.axis_size(axis)
    up = [(i, (i + 1) % size) for i in range(size)]
    before = lax.ppermute(x, axis, up)
    after = lax.ppermute(x, axis, [(j, i) for i, j in up])
    return before, after


def halo(x):
    before, after = both_sides(x, "gy")
    row = jnp.stack([before, x, after])
    before, after = both_sides(row, GX)
    return before, row, after


def shards(
    positions,
    velocity,
    atom_eps,
    neighbours,
    pair_live,
    event_count,
    event_atoms,
    event_weight,
    template_map,
):
    x_size, y_size = lax.axis_size(GX), lax.axis_size("gy")
    z = lax.axis_index("gz").astype(jnp.int32).reshape(1)
    (own,) = call(pack_kernel, [(COLUMN, 48, LANES)], [SMEM] + [VMEM] * 5)(
        event_count, positions, velocity, atom_eps, event_weight, event_atoms
    )
    column = exchanged(own, "gz")
    moved, speeds = call(
        events_kernel,
        [(64, LANES), (48, LANES)],
        [VMEM] * 2,
        [
            pltpu.VMEM((64, LANES), jnp.int32),
            pltpu.VMEM((64, LANES), jnp.int32),
            pltpu.VMEM((9, 64, LANES), F32),
        ],
    )(column, template_map)
    around = halo(moved)
    table = pltpu.VMEM((4, CHUNKS, NEIGH, LANES), F32)
    (pushed,) = call(first_kernel, [(COLUMN, 16, LANES)], [SMEM] + [VMEM] * 6, [table])(
        z, *around, speeds, neighbours, pair_live
    )
    pushed = exchanged(pushed, "gz")
    forces, sums = call(column_kernel, [(96, LANES), (x_size, 1, LANES)], [VMEM] * 2)(
        pushed, speeds
    )
    forces_around = halo(forces)
    sums = exchanged(sums, GX)
    sums = exchanged(added_for_each(sums, y_size), "gy")
    result, sums = call(
        second_kernel,
        [(40, LANES), (x_size * COLUMN, 1, LANES)],
        [SMEM] + [VMEM] * 9,
        [table, pltpu.VMEM((10, 64, LANES), F32)],
    )(z, *around, *forces_around, sums, neighbours, pair_live)
    sums = exchanged(sums, GXZ)
    sums = exchanged(added_for_each(sums, y_size), "gy")
    return tuple(
        call(final_kernel, [positions.shape, velocity.shape], [VMEM] * 2)(result, sums)
    )


def solution(mesh):
    shape = mesh.shape
    split = Mesh(
        mesh.devices.reshape(shape["gx"] // 2, 2, shape["gy"], shape["gz"]),
        ("gx_0", "gx_1", "gy", "gz"),
    )
    in_specs = (
        P(None, GX, "gy", "gz", None),
        P(None, GX, "gy", "gz", None),
        P(GX, "gy", "gz", None),
        P(GX, "gy", "gz", None, None),
        P(GX, "gy", "gz", None, None),
        P(GX, "gy", "gz"),
        P(GX, "gy", "gz", None, None),
        P(GX, "gy", "gz", None),
        P(),
    )
    out_specs = (P(None, GX, "gy", "gz", None), P(None, GX, "gy", "gz", None))
    return jax.shard_map(
        shards, mesh=split, in_specs=in_specs, out_specs=out_specs, check_vma=False
    )
```

time: 369 us -> 141 us (0.38)
  the two profiles are of different devices: /device:TPU:8 before, /device:TPU:1 now
where the time goes in v1:
time: 141 us; the launch traced here: 140 us
  blocking collectives  75.8 us (54%)
  starting transfers between devices  34.6 us (25%)
  Pallas kernels  15.7 us (11%)
  waiting for transfers between devices  9.3 us (7%)
  local copies, waits for them, and re-layouts  1.99 us (1%)
  other arithmetic  1.71 us (1%)
    all_to_all x6, blocking collectives, exchanged(): return lax.all_to_all(x, axes, 0, 0, tiled=True)  75.8 us
    ppermute x4, starting transfers between devices, both_sides(): after = lax.ppermute(x, axis, [(j, i) for i, j in up])  28.1 us
    ppermute x4, waiting for transfers between devices, both_sides(): before = lax.ppermute(x, axis, up)  7.02 us
    ppermute x4, starting transfers between devices, both_sides(): before = lax.ppermute(x, axis, up)  6.5 us
    pallas_call x1, Pallas kernels, shards(): call(events_kernel, [(64, LANES), (48, LANES)], [VMEM] * 2, [pltpu.VMEM((...  6.39 us
  transfers between devices with their start and end apart: 8, of which 3 were waited for; matrix products, arithmetic and copies ran while one was open for 0% of the time, Pallas kernels for 0%

profile of v1, /device:TPU:1, one launch (start us, length us, event | category | flops | bytes accessed | tf_op | source)
XLA Modules:
  0.0 140.4 jit_solution(18196673787243141631)
XLA Ops:
  1.3 1.4 %shard_map.104 = f32[4,48,128]{2,1,0:T(8,128)} custom-call(s32[1,1,1]{2,1,0:T(1,128)S(6)} %copy.11.count_ref, f32[3,1,1,1,512]{4,3,2,1,0:T(1,128)} %pos_ref.1, f32[3,1,1,1,512]{4,3,2,1,0:T(1,128)} %vel_ref.1, f32[1,1,1,512]{3,2,1,0:T(1,128)} %eps_ref.1, f32[1,1,1,16]{3,2,1,0:T(1,128)} %weight_ref.1, s32[1,1,1,16,128]{4,3,2,1,0:T(8,128)} %atoms_ref.1), custom_call_target="tpu_custom_call" | custom-call | flops 10000 | bytes 100000 | tf_op jit(solution)/shard_map/pallas_call | solution.py:291
  2.7 9.6 %all_to_all.30.column_ref = f32[4,48,128]{2,1,0:T(8,128)} all-to-all(f32[4,48,128]{2,1,0:T(8,128)} %shard_map.104), channel_id=1, replica_groups=mesh['gx_0'=8,'gx_1'=2,'gy'=16,'gz'=4] {'gz'}, dimensions={0} | all-to-all | bytes 196608 | tf_op jit(solution)/shard_map/all_to_all | solution.py:256
  12.3 6.4 %shard_map.105 = (f32[64,128]{1,0:T(8,128)}, f32[48,128]{1,0:T(8,128)}) custom-call(f32[4,48,128]{2,1,0:T(8,128)} %all_to_all.30.column_ref, f32[128,128]{1,0:T(8,128)} %map_ref.1), custom_call_target="tpu_custom_call" | custom-call | flops 10000 | bytes 100000 | tf_op jit(solution)/shard_map/pallas_call | solution.py:295
  18.7 17.9 %collective-permute-start.1 = (f32[64,128]{1,0:T(8,128)}, f32[64,128]{1,0:T(8,128)S(1)}, u32[]{:S(2)}, u32[]{:S(2)}) collective-permute-start(f32[64,128]{1,0:T(8,128)} %get-tuple-element.8), channel_id=1, source_target_pairs={{4,0},{8,4},{12,8},{16,12},{20,16},{24,20},{28,24},{32,28},{36,32}... | collective-permute-start | bytes 98312 | tf_op jit(solution)/shard_map/ppermute | solution.py:267
  36.6 1.9 %collective-permute-start = (f32[64,128]{1,0:T(8,128)}, f32[64,128]{1,0:T(8,128)S(1)}, u32[]{:S(2)}, u32[]{:S(2)}) collective-permute-start(f32[64,128]{1,0:T(8,128)} %get-tuple-element.8), channel_id=1, source_target_pairs={{0,4},{4,8},{8,12},{12,16},{16,20},{20,24},{24,28},{28,32},{32,36}... | collective-permute-start | bytes 98312 | tf_op jit(solution)/shard_map/ppermute | solution.py:266
  38.6 0.0 collective-permute-done.1
  38.6 4.1 %collective-permute-done = f32[64,128]{1,0:T(8,128)S(1)} collective-permute-done((f32[64,128]{1,0:T(8,128)}, f32[64,128]{1,0:T(8,128)S(1)}, u32[]{:S(2)}, u32[]{:S(2)}) %collective-permute-start) | collective-permute-done | bytes 32800 | tf_op jit(solution)/shard_map/ppermute | solution.py:266
  42.7 0.8 pad_maximum_fusion.1.o_ref
  43.5 0.0 copy-start
  43.5 3.5 %collective-permute-start.3 = (f32[3,64,128]{2,1,0:T(8,128)S(1)}, f32[3,64,128]{2,1,0:T(8,128)S(1)}, u32[]{:S(2)}, u32[]{:S(2)}) collective-permute-start(f32[3,64,128]{2,1,0:T(8,128)S(1)} %pad_maximum_fusion.1.o_ref), channel_id=1, source_target_pairs={{64,0},{128,64},{192,128},{256,192},{320,256},{384,320},{448,384},... | collective-permute-start | bytes 294920 | tf_op jit(solution)/shard_map/ppermute | solution.py:267
  47.0 1.2 collective-permute-start.2
  48.3 2.3 %collective-permute-done.3.p_ref = f32[3,64,128]{2,1,0:T(8,128)S(1)} collective-permute-done((f32[3,64,128]{2,1,0:T(8,128)S(1)}, f32[3,64,128]{2,1,0:T(8,128)S(1)}, u32[]{:S(2)}, u32[]{:S(2)}) %collective-permute-start.3) | collective-permute-done | bytes 98336 | tf_op jit(solution)/shard_map/ppermute | solution.py:267
  50.5 0.0 copy-start.2
  50.5 0.0 collective-permute-done.2.m_ref
  50.5 0.0 copy-start.3
  50.5 0.0 copy-done
  50.5 0.6 copy-done.2
  51.2 0.0 copy-done.3
  51.2 2.3 %shard_map.106 = f32[4,16,128]{2,1,0:T(8,128)} custom-call(s32[1]{0:T(128)} %bitcast.z_ref, f32[3,64,128]{2,1,0:T(8,128)} %copy-done.3, f32[3,64,128]{2,1,0:T(8,128)} %copy-done, f32[3,64,128]{2,1,0:T(8,128)} %copy-done.2, f32[48,128]{1,0:T(8,128)} %get-tuple-element.9.vel_ref, s32[1,1,1,32,512]{4,3,2,1,0:T(8,128)} %neigh_ref.3, s32[1,1,1,32,512]{4,3,2,1,0:T(8,128)} %live_ref.3), custom_call_target="tpu_custom_call" | custom-call | flops 10000 | bytes 100000 | tf_op jit(solution)/shard_map/pallas_call | solution.py:307
  53.5 8.2 %all_to_all.31.parts_ref = f32[4,16,128]{2,1,0:T(8,128)} all-to-all(f32[4,16,128]{2,1,0:T(8,128)} %shard_map.106), channel_id=1, replica_groups=mesh['gx_0'=8,'gx_1'=2,'gy'=16,'gz'=4] {'gz'}, dimensions={0} | all-to-all | bytes 65536 | tf_op jit(solution)/shard_map/all_to_all | solution.py:256
  61.7 1.4 shard_map.107
  63.1 1.9 %collective-permute-start.5 = (f32[96,128]{1,0:T(8,128)}, f32[96,128]{1,0:T(8,128)S(1)}, u32[]{:S(2)}, u32[]{:S(2)}) collective-permute-start(f32[96,128]{1,0:T(8,128)} %get-tuple-element.10), channel_id=1, source_target_pairs={{4,0},{8,4},{12,8},{16,12},{20,16},{24,20},{28,24},{32,28},{36,32}... | collective-permute-start | bytes 147464 | tf_op jit(solution)/shard_map/ppermute | solution.py:267
  65.0 3.4 %collective-permute-start.4 = (f32[96,128]{1,0:T(8,128)}, f32[96,128]{1,0:T(8,128)S(1)}, u32[]{:S(2)}, u32[]{:S(2)}) collective-permute-start(f32[96,128]{1,0:T(8,128)} %get-tuple-element.10), channel_id=1, source_target_pairs={{0,4},{4,8},{8,12},{12,16},{16,20},{20,24},{24,28},{28,32},{32,36}... | collective-permute-start | bytes 147464 | tf_op jit(solution)/shard_map/ppermute | solution.py:266
  68.4 0.0 collective-permute-done.5
  68.4 2.9 %collective-permute-done.4 = f32[96,128]{1,0:T(8,128)S(1)} collective-permute-done((f32[96,128]{1,0:T(8,128)}, f32[96,128]{1,0:T(8,128)S(1)}, u32[]{:S(2)}, u32[]{:S(2)}) %collective-permute-start.4) | collective-permute-done | bytes 49184 | tf_op jit(solution)/shard_map/ppermute | solution.py:266
  71.3 0.0 copy-start.6
  71.3 0.8 pad_maximum_fusion.fo_ref
  72.1 0.0 copy-start.1
  72.1 4.7 %collective-permute-start.7 = (f32[3,96,128]{2,1,0:T(8,128)S(1)}, f32[3,96,128]{2,1,0:T(8,128)S(1)}, u32[]{:S(2)}, u32[]{:S(2)}) collective-permute-start(f32[3,96,128]{2,1,0:T(8,128)S(1)} %pad_maximum_fusion.fo_ref), channel_id=1, source_target_pairs={{64,0},{128,64},{192,128},{256,192},{320,256},{384,320},{448,384},... | collective-permute-start | bytes 442376 | tf_op jit(solution)/shard_map/ppermute | solution.py:267
  76.8 0.0 collective-permute-start.6
  76.8 0.0 copy-done.6
  76.8 13.8 %all_to_all.32 = f32[16,1,128]{2,1,0:T(1,128)S(1)} all-to-all(f32[16,1,128]{2,1,0:T(1,128)S(1)} %copy-done.6), channel_id=1, replica_groups=mesh['gx_0'=8,'gx_1'=2,'gy'=16,'gz'=4] {'gx_0','gx_1'}, dimensions={0} | all-to-all | bytes 16384 | tf_op jit(solution)/shard_map/all_to_all | solution.py:256
  90.7 14.3 %all_to_all.33.sums_ref = f32[16,1,128]{2,1,0:T(1,128)} all-to-all(f32[16,1,128]{2,1,0:T(1,128)S(1)} %broadcast_in_dim.4), channel_id=1, replica_groups=mesh['gx_0'=8,'gx_1'=2,'gy'=16,'gz'=4] {'gy'}, dimensions={0} | all-to-all | bytes 16384 | tf_op jit(solution)/shard_map/all_to_all | solution.py:256
  105.0 0.0 collective-permute-done.7.fp_ref
  105.0 0.0 copy-start.4
  105.0 0.0 collective-permute-done.6.fm_ref
  105.0 0.0 copy-done.1
  105.0 0.6 copy-done.4
  105.6 0.0 copy-start.5
  105.6 0.7 copy-done.5
  106.3 2.7 %shard_map.108 = (f32[40,128]{1,0:T(8,128)}, f32[64,1,128]{2,1,0:T(1,128)}) custom-call(s32[1]{0:T(128)} %bitcast.z_ref, f32[3,64,128]{2,1,0:T(8,128)} %copy-done.3, f32[3,64,128]{2,1,0:T(8,128)} %copy-done, f32[3,64,128]{2,1,0:T(8,128)} %copy-done.2, f32[3,96,128]{2,1,0:T(8,128)} %copy-done.5, f32[3,96,128]{2,1,0:T(8,128)} %copy-done.1, ...), custom_call_target="tpu_custom_call" | custom-call | flops 10000 | bytes 100000 | tf_op jit(solution)/shard_map/pallas_call | solution.py:317
  109.0 15.4 %all_to_all.34 = f32[64,1,128]{2,1,0:T(1,128)S(1)} all-to-all(f32[64,1,128]{2,1,0:T(1,128)} %get-tuple-element.13), channel_id=1, replica_groups=mesh['gx_0'=8,'gx_1'=2,'gy'=16,'gz'=4] {'gx_0','gx_1','gz'}, dimensions={0} | all-to-all | bytes 65536 | tf_op jit(solution)/shard_map/all_to_all | solution.py:256
  124.4 0.1 reduce_sum.19
  124.5 14.5 %all_to_all.35.sums_ref = f32[16,1,128]{2,1,0:T(1,128)} all-to-all(f32[16,1,128]{2,1,0:T(1,128)S(1)} %broadcast_in_dim.5), channel_id=1, replica_groups=mesh['gx_0'=8,'gx_1'=2,'gy'=16,'gz'=4] {'gy'}, dimensions={0} | all-to-all | bytes 16384 | tf_op jit(solution)/shard_map/all_to_all | solution.py:256
  139.0 1.5 %shard_map.109 = (f32[3,1,1,1,512]{4,3,2,1,0:T(1,128)}, f32[3,1,1,1,512]{4,3,2,1,0:T(1,128)}) custom-call(f32[40,128]{1,0:T(8,128)} %get-tuple-element.12.own_ref, f32[16,1,128]{2,1,0:T(1,128)} %all_to_all.35.sums_ref), custom_call_target="tpu_custom_call" | custom-call | flops 10000 | bytes 100000 | tf_op jit(solution)/shard_map/pallas_call | solution.py:326
  (3 shorter events, 0.1 us)
Async XLA Ops:
  18.7 19.9 %collective-permute-start.1 = (f32[64,128]{1,0:T(8,128)}, f32[64,128]{1,0:T(8,128)S(1)}, u32[]{:S(2)}, u32[]{:S(2)}) collective-permute-start(f32[64,128]{1,0:T(8,128)} %get-tuple-element.8), channel_id=1, source_target_pairs={{4,0},{8,4},{12,8},{16,12},{20,16},{24,20},{28,24},{32,28},{36,32}... | collective-permute-start | bytes 98312 | tf_op jit(solution)/shard_map/ppermute | solution.py:267
  36.6 6.1 %collective-permute-start = (f32[64,128]{1,0:T(8,128)}, f32[64,128]{1,0:T(8,128)S(1)}, u32[]{:S(2)}, u32[]{:S(2)}) collective-permute-start(f32[64,128]{1,0:T(8,128)} %get-tuple-element.8), channel_id=1, source_target_pairs={{0,4},{4,8},{8,12},{12,16},{16,20},{20,24},{24,28},{28,32},{32,36}... | collective-permute-start | bytes 98312 | tf_op jit(solution)/shard_map/ppermute | solution.py:266
  43.5 7.1 %copy-start = (f32[3,64,128]{2,1,0:T(8,128)}, f32[3,64,128]{2,1,0:T(8,128)S(1)}, u32[]{:S(2)}) copy-start(f32[3,64,128]{2,1,0:T(8,128)S(1)} %pad_maximum_fusion.1.o_ref) | copy-start | bytes 294916
  43.5 7.0 %collective-permute-start.3 = (f32[3,64,128]{2,1,0:T(8,128)S(1)}, f32[3,64,128]{2,1,0:T(8,128)S(1)}, u32[]{:S(2)}, u32[]{:S(2)}) collective-permute-start(f32[3,64,128]{2,1,0:T(8,128)S(1)} %pad_maximum_fusion.1.o_ref), channel_id=1, source_target_pairs={{64,0},{128,64},{192,128},{256,192},{320,256},{384,320},{448,384},... | collective-permute-start | bytes 294920 | tf_op jit(solution)/shard_map/ppermute | solution.py:267
  47.0 3.5 %collective-permute-start.2 = (f32[3,64,128]{2,1,0:T(8,128)S(1)}, f32[3,64,128]{2,1,0:T(8,128)S(1)}, u32[]{:S(2)}, u32[]{:S(2)}) collective-permute-start(f32[3,64,128]{2,1,0:T(8,128)S(1)} %pad_maximum_fusion.1.o_ref), channel_id=1, source_target_pairs={{0,64},{64,128},{128,192},{192,256},{256,320},{320,384},{384,448},... | collective-permute-start | bytes 294920 | tf_op jit(solution)/shard_map/ppermute | solution.py:266
  50.5 0.6 copy-start.2
  50.5 0.7 copy-start.3
  63.1 5.3 %collective-permute-start.5 = (f32[96,128]{1,0:T(8,128)}, f32[96,128]{1,0:T(8,128)S(1)}, u32[]{:S(2)}, u32[]{:S(2)}) collective-permute-start(f32[96,128]{1,0:T(8,128)} %get-tuple-element.10), channel_id=1, source_target_pairs={{4,0},{8,4},{12,8},{16,12},{20,16},{24,20},{28,24},{32,28},{36,32}... | collective-permute-start | bytes 147464 | tf_op jit(solution)/shard_map/ppermute | solution.py:267
  65.0 6.3 %collective-permute-start.4 = (f32[96,128]{1,0:T(8,128)}, f32[96,128]{1,0:T(8,128)S(1)}, u32[]{:S(2)}, u32[]{:S(2)}) collective-permute-start(f32[96,128]{1,0:T(8,128)} %get-tuple-element.10), channel_id=1, source_target_pairs={{0,4},{4,8},{8,12},{12,16},{16,20},{20,24},{24,28},{28,32},{32,36}... | collective-permute-start | bytes 147464 | tf_op jit(solution)/shard_map/ppermute | solution.py:266
  71.3 5.5 %copy-start.6 = (f32[16,1,128]{2,1,0:T(1,128)S(1)}, f32[16,1,128]{2,1,0:T(1,128)}, u32[]{:S(2)}) copy-start(f32[16,1,128]{2,1,0:T(1,128)} %get-tuple-element.11) | copy-start | bytes 24580
  72.1 32.9 %copy-start.1 = (f32[3,96,128]{2,1,0:T(8,128)}, f32[3,96,128]{2,1,0:T(8,128)S(1)}, u32[]{:S(2)}) copy-start(f32[3,96,128]{2,1,0:T(8,128)S(1)} %pad_maximum_fusion.fo_ref) | copy-start | bytes 442372
  72.1 32.9 %collective-permute-start.7 = (f32[3,96,128]{2,1,0:T(8,128)S(1)}, f32[3,96,128]{2,1,0:T(8,128)S(1)}, u32[]{:S(2)}, u32[]{:S(2)}) collective-permute-start(f32[3,96,128]{2,1,0:T(8,128)S(1)} %pad_maximum_fusion.fo_ref), channel_id=1, source_target_pairs={{64,0},{128,64},{192,128},{256,192},{320,256},{384,320},{448,384},... | collective-permute-start | bytes 442376 | tf_op jit(solution)/shard_map/ppermute | solution.py:267
  76.8 28.2 %collective-permute-start.6 = (f32[3,96,128]{2,1,0:T(8,128)S(1)}, f32[3,96,128]{2,1,0:T(8,128)S(1)}, u32[]{:S(2)}, u32[]{:S(2)}) collective-permute-start(f32[3,96,128]{2,1,0:T(8,128)S(1)} %pad_maximum_fusion.fo_ref), channel_id=1, source_target_pairs={{0,64},{64,128},{128,192},{192,256},{256,320},{320,384},{384,448},... | collective-permute-start | bytes 442376 | tf_op jit(solution)/shard_map/ppermute | solution.py:266
  105.0 0.7 copy-start.4
  105.6 0.7 copy-start.5

commit v2 on v1

--- a/solution.py
+++ b/solution.py
@@ -13,6 +13,7 @@
 GXZ = ("gx_0", "gx_1", "gz")
 COLUMN = 4
 CHUNKS = 4
+LIVE = 32
 LANES = 128
 F32 = jnp.float32
 
@@ -23,25 +24,45 @@
 
 SMEM = pl.BlockSpec(memory_space=pltpu.SMEM)
 VMEM = pl.BlockSpec(memory_space=pltpu.VMEM)
-
-
-def call(kernel, outs, specs, scratch=(), flops=10000):
+HBM = pl.BlockSpec(memory_space=pltpu.HBM)
+
+
+def call(kernel, outs, specs, scratch=(), limit=4 << 20):
     return pl.pallas_call(
         kernel,
         out_shape=[jax.ShapeDtypeStruct(shape, F32) for shape in outs],
         in_specs=specs,
         out_specs=[VMEM] * len(outs),
         scratch_shapes=list(scratch),
-        cost_estimate=pl.CostEstimate(flops=flops, bytes_accessed=100000, transcendentals=0),
-    )
-
-
-def pack_kernel(count_ref, pos_ref, vel_ref, eps_ref, weight_ref, atoms_ref, out_ref):
-    live = lax.broadcasted_iota(jnp.int32, (1, EV_DEV), 1) < count_ref[0, 0, 0]
+        cost_estimate=pl.CostEstimate(flops=10000, bytes_accessed=100000, transcendentals=0),
+        compiler_params=pltpu.CompilerParams(vmem_limit_bytes=limit),
+    )
+
+
+def pack_kernel(
+    count_ref, pos_hbm, vel_hbm, eps_hbm, weight_hbm, atoms_hbm, out_ref,
+    pos_ref, vel_ref, eps_ref, weight_ref, atoms_ref, sems,
+):
+    pairs = (
+        (pos_hbm, pos_ref),
+        (vel_hbm, vel_ref),
+        (eps_hbm, eps_ref),
+        (weight_hbm, weight_ref),
+        (atoms_hbm, atoms_ref),
+    )
+    copies = [pltpu.make_async_copy(*pair, sems.at[n]) for n, pair in enumerate(pairs)]
+    for copy in copies:
+        copy.start()
+    for copy in range(COLUMN):
+        out_ref[copy, 24:32, :] = jnp.zeros((8, LANES), F32)
+    for copy in copies:
+        copy.wait()
+    count = count_ref[0, 0, 0]
+    live = lax.broadcasted_iota(jnp.int32, (1, EV_DEV), 1) < count
     weights = jnp.where(live, weight_ref[0, 0, :, :], 0.0)
+    counts = jnp.full((1, LANES), count, jnp.int32).astype(F32)
     atoms = atoms_ref[0, 0, 0, :, :].astype(F32)
     for copy in range(COLUMN):
-        out_ref[copy, 24:32, :] = jnp.zeros((8, LANES), F32)
         for c in range(3):
             for q in range(CHUNKS):
                 cut = pl.ds(q * LANES, LANES)
@@ -50,31 +71,33 @@
         for q in range(CHUNKS):
             out_ref[copy, 12 + q : 13 + q, :] = eps_ref[0, 0, :, pl.ds(q * LANES, LANES)]
         out_ref[copy, 28:29, 0:EV_DEV] = weights
+        out_ref[copy, 29:30, :] = counts
         out_ref[copy, 32:48, :] = atoms
 
 
-def events_kernel(column_ref, map_ref, moved_ref, vel_ref, low_ref, high_ref, shift_ref):
-    slots = COLUMN * EV_DEV
-    atoms = jnp.concatenate([column_ref[z, 32:48, :] for z in range(COLUMN)], 0).astype(jnp.int32)
+def events_kernel(column_ref, map_ref, moved_ref, vel_ref, atoms_ref, low_ref, high_ref, shift_ref):
+    atoms_ref[...] = jnp.zeros(atoms_ref.shape, F32)
+    first = jnp.int32(0)
+    lane_weights = jnp.zeros((1, LANES), F32)
+    for z in range(COLUMN):
+        for e in range(EV_DEV):
+            atoms_ref[pl.ds(first + e, 1), :] = column_ref[z, 32 + e : 33 + e, :]
+        lane_weights = lane_weights + pltpu.roll(column_ref[z, 28:29, :], first, 1)
+        if z < COLUMN - 1:
+            first = first + jnp.max(column_ref[z, 29:30, :]).astype(jnp.int32)
+    atoms = atoms_ref[0:LIVE, :].astype(jnp.int32)
     low, high = atoms & (LANES - 1), atoms >> 7
     low_ref[...] = low
     high_ref[...] = high
-    diagonal = lax.broadcasted_iota(jnp.int32, (EV_DEV, LANES), 0) == lax.broadcasted_iota(
-        jnp.int32, (EV_DEV, LANES), 1
-    )
-    weights = jnp.concatenate(
-        [
-            jnp.sum(jnp.where(diagonal, column_ref[z, 28:29, :], 0.0), axis=1, keepdims=True)
-            for z in range(COLUMN)
-        ],
-        0,
-    )
+    slot = lax.broadcasted_iota(jnp.int32, (LIVE, LANES), 0)
+    lane = lax.broadcasted_iota(jnp.int32, (LIVE, LANES), 1)
+    weights = jnp.sum(jnp.where(slot == lane, lane_weights, 0.0), axis=1, keepdims=True)
     centred = []
     for c in range(3):
-        taken = jnp.zeros((slots, LANES), F32)
+        taken = jnp.zeros((LIVE, LANES), F32)
         for h in range(COLUMN * CHUNKS):
             z, q = divmod(h, CHUNKS)
-            row = jnp.broadcast_to(column_ref[z, c * 4 + q : c * 4 + q + 1, :], (slots, LANES))
+            row = jnp.broadcast_to(column_ref[z, c * 4 + q : c * 4 + q + 1, :], (LIVE, LANES))
             taken = jnp.where(high == h, jnp.take_along_axis(row, low, axis=1), taken)
         centred.append(taken - jnp.sum(taken, axis=1, keepdims=True) * (1.0 / TEMPLATE))
     shift = jnp.dot(
@@ -87,27 +110,25 @@
     for part in range(3):
         rounded = shift.astype(jnp.bfloat16).astype(F32)
         for c in range(3):
-            shift_ref[part * 3 + c, :, :] = rounded[c * slots : (c + 1) * slots]
+            shift_ref[part * 3 + c, :, :] = rounded[c * LIVE : (c + 1) * LIVE]
         shift = shift - rounded
     places = lax.broadcasted_iota(jnp.int32, (LANES, LANES), 0)
     rows = lax.broadcasted_iota(jnp.int32, (16, LANES), 0)
-
-    def some_events(i, total):
+    total = jnp.zeros((144, LANES), F32)
+    for i in range(LIVE // 4):
         lefts, rights = [], []
         for j in range(4):
-            e = pl.ds(i * 4 + j, 1)
+            e = slice(i * 4 + j, i * 4 + j + 1)
             here = high_ref[e, :] == rows
             left = [jnp.where(here, shift_ref[n, e, :], 0.0) for n in range(9)]
             lefts.append(jnp.concatenate(left, 0).astype(jnp.bfloat16))
             rights.append(jnp.where(low_ref[e, :] == places, 1.0, 0.0).astype(jnp.bfloat16))
-        return total + lax.dot_general(
+        total = total + lax.dot_general(
             jnp.concatenate(lefts, 1),
             jnp.concatenate(rights, 1),
             (((1,), (1,)), ((), ())),
             preferred_element_type=F32,
         )
-
-    total = lax.fori_loop(0, slots // 4, some_events, jnp.zeros((144, LANES), F32))
     displaced = total[0:48] + total[48:96] + total[96:144]
     for z in range(COLUMN):
         for c in range(3):
@@ -268,8 +289,7 @@
     return before, after
 
 
-def halo(x):
-    before, after = both_sides(x, "gy")
+def joined(before, x, after):
     row = jnp.stack([before, x, after])
     before, after = both_sides(row, GX)
     return before, row, after
@@ -288,21 +308,24 @@
 ):
     x_size, y_size = lax.axis_size(GX), lax.axis_size("gy")
     z = lax.axis_index("gz").astype(jnp.int32).reshape(1)
-    (own,) = call(pack_kernel, [(COLUMN, 48, LANES)], [SMEM] + [VMEM] * 5)(
-        event_count, positions, velocity, atom_eps, event_weight, event_atoms
-    )
+    inputs = (event_count, positions, velocity, atom_eps, event_weight, event_atoms)
+    staged = [pltpu.VMEM(x.shape, x.dtype) for x in inputs[1:]]
+    staged += [pltpu.SemaphoreType.DMA((len(staged),))]
+    (own,) = call(pack_kernel, [(COLUMN, 48, LANES)], [SMEM] + [HBM] * 5, staged, None)(*inputs)
     column = exchanged(own, "gz")
     moved, speeds = call(
         events_kernel,
         [(64, LANES), (48, LANES)],
         [VMEM] * 2,
         [
-            pltpu.VMEM((64, LANES), jnp.int32),
-            pltpu.VMEM((64, LANES), jnp.int32),
-            pltpu.VMEM((9, 64, LANES), F32),
+            pltpu.VMEM((LIVE + EV_DEV, LANES), F32),
+            pltpu.VMEM((LIVE, LANES), jnp.int32),
+            pltpu.VMEM((LIVE, LANES), jnp.int32),
+            pltpu.VMEM((9, LIVE, LANES), F32),
         ],
     )(column, template_map)
-    around = halo(moved)
+    before, after = both_sides(moved, "gy")
+    around = joined(before, moved, after)
     table = pltpu.VMEM((4, CHUNKS, NEIGH, LANES), F32)
     (pushed,) = call(first_kernel, [(COLUMN, 16, LANES)], [SMEM] + [VMEM] * 6, [table])(
         z, *around, speeds, neighbours, pair_live
@@ -311,8 +334,10 @@
     forces, sums = call(column_kernel, [(96, LANES), (x_size, 1, LANES)], [VMEM] * 2)(
         pushed, speeds
     )
-    forces_around = halo(forces)
+    before, after = both_sides(forces, "gy")
     sums = exchanged(sums, GX)
+    before, after, sums = lax.optimization_barrier((before, after, sums))
+    forces_around = joined(before, forces, after)
     sums = exchanged(added_for_each(sums, y_size), "gy")
     result, sums = call(
         second_kernel,

time: 141 us -> 122 us (0.87)
  Pallas kernels: 15.7 us -> 5.24 us
  waiting for transfers between devices: 9.3 us -> 6.22 us
  starting transfers between devices: 34.6 us -> 31.7 us
  local copies, waits for them, and re-layouts: 1.99 us -> 0.03 us
  other arithmetic: 1.71 us -> 0.14 us
    pallas_call x1, Pallas kernels: 6.39 us -> 1.48 us  [shards(): call(events_kernel, [(64, LANES), (48, LANES)], [VMEM] * 2, [pltpu.VMEM((...]
    ppermute x4, starting transfers between devices: 28.1 us -> 24.1 us  [both_sides(): after = lax.ppermute(x, axis, [(j, i) for i, j in up])]
    ppermute x4, waiting for transfers between devices: 7.02 us -> 3.94 us  [both_sides(): before = lax.ppermute(x, axis, up)]
    unnamed x14 -> x6, local copies, waits for them, and re-layouts: 1.97 us -> 0.01 us
    pallas_call x1, Pallas kernels: 2.73 us -> 0.9 us  [shards(): call(second_kernel, [(40, LANES), (x_size * COLUMN, 1, LANES)], [SMEM] +...]
    pallas_call x1, Pallas kernels: 2.29 us -> 0.66 us  [shards(): call(first_kernel, [(COLUMN, 16, LANES)], [SMEM] + [VMEM] * 6, [table])]
    another operation x2, other arithmetic: 1.59 us -> 0.02 us  [joined(): row = jnp.stack([before, x, after])]
  transfers between devices with their start and end apart: 8 -> 8, of which waited for: 3 -> 2; matrix products, arithmetic and copies ran while one was open for 0% -> 0% of each run, Pallas kernels for 0% -> 0%
where the time goes in v2:
time: 122 us; the launch traced here: 121 us
  blocking collectives  76.7 us (63%)
  starting transfers between devices  31.7 us (26%)
  waiting for transfers between devices  6.22 us (5%)
  Pallas kernels  5.24 us (4%)
  between operations  1.38 us (1%)
    all_to_all x6, blocking collectives, exchanged(): return lax.all_to_all(x, axes, 0, 0, tiled=True)  76.7 us
    ppermute x4, starting transfers between devices, both_sides(): after = lax.ppermute(x, axis, [(j, i) for i, j in up])  24.1 us
    ppermute x4, starting transfers between devices, both_sides(): before = lax.ppermute(x, axis, up)  7.58 us
    ppermute x4, waiting for transfers between devices, both_sides(): before = lax.ppermute(x, axis, up)  3.94 us
  transfers between devices with their start and end apart: 8, of which 2 were waited for; matrix products, arithmetic and copies ran while one was open for 0% of the time, Pallas kernels for 0%

profile of v2, /device:TPU:1, one launch (start us, length us, event | category | flops | bytes accessed | tf_op | source)
XLA Modules:
  0.0 121.3 jit_solution(7275441440136388008)
XLA Ops:
  1.3 1.5 %shard_map.104 = f32[4,48,128]{2,1,0:T(8,128)} custom-call(s32[1,1,1]{2,1,0:T(1,128)S(6)} %copy.11.count_ref, f32[3,1,1,1,512]{4,3,2,1,0:T(1,128)} %pos_hbm.1, f32[3,1,1,1,512]{4,3,2,1,0:T(1,128)} %vel_hbm.1, f32[1,1,1,512]{3,2,1,0:T(1,128)} %eps_hbm.1, f32[1,1,1,16]{3,2,1,0:T(1,128)} %weight_hbm.1, s32[1,1,1,16,128]{4,3,2,1,0:T(8,128)} %atoms_hbm.1), custom_call_target="tpu_custom_call" | custom-call | flops 10000 | bytes 100000 | tf_op jit(solution)/shard_map/pallas_call | solution.py:314
  2.8 0.0 copy-start.2
  2.8 9.6 %all_to_all.30.column_ref = f32[4,48,128]{2,1,0:T(8,128)S(1)} all-to-all(f32[4,48,128]{2,1,0:T(8,128)} %shard_map.104), channel_id=1, replica_groups=mesh['gx_0'=8,'gx_1'=2,'gy'=16,'gz'=4] {'gz'}, dimensions={0} | all-to-all | bytes 196608 | tf_op jit(solution)/shard_map/all_to_all | solution.py:277
  12.4 0.0 copy-done.2
  12.4 1.5 %shard_map.105 = (f32[64,128]{1,0:T(8,128)S(1)}, f32[48,128]{1,0:T(8,128)S(1)}) custom-call(f32[4,48,128]{2,1,0:T(8,128)S(1)} %all_to_all.30.column_ref, f32[128,128]{1,0:T(8,128)S(1)} %copy-done.2), custom_call_target="tpu_custom_call" | custom-call | flops 10000 | bytes 100000 | tf_op jit(solution)/shard_map/pallas_call | solution.py:316
  13.9 17.9 %collective-permute-start.1 = (f32[64,128]{1,0:T(8,128)S(1)}, f32[64,128]{1,0:T(8,128)S(1)}, u32[]{:S(2)}, u32[]{:S(2)}) collective-permute-start(f32[64,128]{1,0:T(8,128)S(1)} %get-tuple-element.11), channel_id=1, source_target_pairs={{4,0},{8,4},{12,8},{16,12},{20,16},{24,20},{28,24},{32,28},{36,32}... | collective-permute-start | bytes 98312 | tf_op jit(solution)/shard_map/ppermute | solution.py:288
  31.8 1.9 %collective-permute-start = (f32[64,128]{1,0:T(8,128)S(1)}, f32[64,128]{1,0:T(8,128)S(1)}, u32[]{:S(2)}, u32[]{:S(2)}) collective-permute-start(f32[64,128]{1,0:T(8,128)S(1)} %get-tuple-element.11), channel_id=1, source_target_pairs={{0,4},{4,8},{8,12},{12,16},{16,20},{20,24},{24,28},{28,32},{32,36}... | collective-permute-start | bytes 98312 | tf_op jit(solution)/shard_map/ppermute | solution.py:287
  33.8 0.0 collective-permute-done.1
  33.8 3.9 %collective-permute-done = f32[64,128]{1,0:T(8,128)S(1)} collective-permute-done((f32[64,128]{1,0:T(8,128)S(1)}, f32[64,128]{1,0:T(8,128)S(1)}, u32[]{:S(2)}, u32[]{:S(2)}) %collective-permute-start) | collective-permute-done | bytes 32800 | tf_op jit(solution)/shard_map/ppermute | solution.py:287
  37.7 0.0 copy-start
  37.7 0.0 copy-start.1
  37.7 3.5 %collective-permute-start.3 = (f32[3,64,128]{2,1,0:T(8,128)S(1)}, f32[3,64,128]{2,1,0:T(8,128)S(1)}, u32[]{:S(2)}, u32[]{:S(2)}) collective-permute-start(f32[3,64,128]{2,1,0:T(8,128)S(1)} %pad_maximum_fusion.1.o_ref), channel_id=1, source_target_pairs={{64,0},{128,64},{192,128},{256,192},{320,256},{384,320},{448,384},... | collective-permute-start | bytes 294920 | tf_op jit(solution)/shard_map/ppermute | solution.py:288
  41.3 1.2 collective-permute-start.2
  42.5 2.3 %collective-permute-done.3.p_ref = f32[3,64,128]{2,1,0:T(8,128)S(1)} collective-permute-done((f32[3,64,128]{2,1,0:T(8,128)S(1)}, f32[3,64,128]{2,1,0:T(8,128)S(1)}, u32[]{:S(2)}, u32[]{:S(2)}) %collective-permute-start.3) | collective-permute-done | bytes 98336 | tf_op jit(solution)/shard_map/ppermute | solution.py:288
  44.8 0.0 collective-permute-done.2.m_ref
  44.8 0.0 copy-done
  44.8 0.0 copy-done.1
  44.8 0.7 shard_map.106
  45.4 6.6 %all_to_all.31.parts_ref = f32[4,16,128]{2,1,0:T(8,128)S(1)} all-to-all(f32[4,16,128]{2,1,0:T(8,128)S(1)} %shard_map.106), channel_id=1, replica_groups=mesh['gx_0'=8,'gx_1'=2,'gy'=16,'gz'=4] {'gz'}, dimensions={0} | all-to-all | bytes 65536 | tf_op jit(solution)/shard_map/all_to_all | solution.py:277
  52.1 1.9 %collective-permute-start.5 = (f32[96,128]{1,0:T(8,128)S(1)}, f32[96,128]{1,0:T(8,128)S(1)}, u32[]{:S(2)}, u32[]{:S(2)}) collective-permute-start(f32[96,128]{1,0:T(8,128)S(1)} %get-tuple-element.13), channel_id=1, source_target_pairs={{4,0},{8,4},{12,8},{16,12},{20,16},{24,20},{28,24},{32,28},{36,32}... | collective-permute-start | bytes 147464 | tf_op jit(solution)/shard_map/ppermute | solution.py:288
  54.0 3.4 %collective-permute-start.4 = (f32[96,128]{1,0:T(8,128)S(1)}, f32[96,128]{1,0:T(8,128)S(1)}, u32[]{:S(2)}, u32[]{:S(2)}) collective-permute-start(f32[96,128]{1,0:T(8,128)S(1)} %get-tuple-element.13), channel_id=1, source_target_pairs={{0,4},{4,8},{8,12},{12,16},{16,20},{20,24},{24,28},{28,32},{32,36}... | collective-permute-start | bytes 147464 | tf_op jit(solution)/shard_map/ppermute | solution.py:287
  57.4 17.4 %all_to_all.32 = f32[16,1,128]{2,1,0:T(1,128)S(1)} all-to-all(f32[16,1,128]{2,1,0:T(1,128)S(1)} %get-tuple-element.14), channel_id=1, replica_groups=mesh['gx_0'=8,'gx_1'=2,'gy'=16,'gz'=4] {'gx_0','gx_1'}, dimensions={0} | all-to-all | bytes 16384 | tf_op jit(solution)/shard_map/all_to_all | solution.py:277
  74.8 0.0 collective-permute-done.5
  74.8 0.0 collective-permute-done.4
  74.9 0.7 collective-permute-start.7
  75.5 1.1 collective-permute-start.6
  76.7 14.6 %all_to_all.33.sums_ref = f32[16,1,128]{2,1,0:T(1,128)S(1)} all-to-all(f32[16,1,128]{2,1,0:T(1,128)S(1)} %broadcast_in_dim.4), channel_id=1, replica_groups=mesh['gx_0'=8,'gx_1'=2,'gy'=16,'gz'=4] {'gy'}, dimensions={0} | all-to-all | bytes 16384 | tf_op jit(solution)/shard_map/all_to_all | solution.py:277
  91.3 0.0 collective-permute-done.7.fp_ref
  91.3 0.0 collective-permute-done.6.fm_ref
  91.3 0.9 shard_map.108
  92.2 14.5 %all_to_all.34 = f32[64,1,128]{2,1,0:T(1,128)S(1)} all-to-all(f32[64,1,128]{2,1,0:T(1,128)S(1)} %get-tuple-element.19), channel_id=1, replica_groups=mesh['gx_0'=8,'gx_1'=2,'gy'=16,'gz'=4] {'gx_0','gx_1','gz'}, dimensions={0} | all-to-all | bytes 65536 | tf_op jit(solution)/shard_map/all_to_all | solution.py:277
  106.7 0.1 reduce_sum.19
  106.8 13.8 %all_to_all.35.sums_ref = f32[16,1,128]{2,1,0:T(1,128)S(1)} all-to-all(f32[16,1,128]{2,1,0:T(1,128)S(1)} %broadcast_in_dim.5), channel_id=1, replica_groups=mesh['gx_0'=8,'gx_1'=2,'gy'=16,'gz'=4] {'gy'}, dimensions={0} | all-to-all | bytes 16384 | tf_op jit(solution)/shard_map/all_to_all | solution.py:277
  120.6 0.7 shard_map.109
  (6 shorter events, 0.1 us)
Async XLA Ops:
  2.8 9.6 %copy-start.2 = (f32[128,128]{1,0:T(8,128)S(1)}, f32[128,128]{1,0:T(8,128)}, u32[]{:S(2)}) copy-start(f32[128,128]{1,0:T(8,128)} %map_ref.1) | copy-start | bytes 196612
  13.9 19.9 %collective-permute-start.1 = (f32[64,128]{1,0:T(8,128)S(1)}, f32[64,128]{1,0:T(8,128)S(1)}, u32[]{:S(2)}, u32[]{:S(2)}) collective-permute-start(f32[64,128]{1,0:T(8,128)S(1)} %get-tuple-element.11), channel_id=1, source_target_pairs={{4,0},{8,4},{12,8},{16,12},{20,16},{24,20},{28,24},{32,28},{36,32}... | collective-permute-start | bytes 98312 | tf_op jit(solution)/shard_map/ppermute | solution.py:288
  31.8 5.9 %collective-permute-start = (f32[64,128]{1,0:T(8,128)S(1)}, f32[64,128]{1,0:T(8,128)S(1)}, u32[]{:S(2)}, u32[]{:S(2)}) collective-permute-start(f32[64,128]{1,0:T(8,128)S(1)} %get-tuple-element.11), channel_id=1, source_target_pairs={{0,4},{4,8},{8,12},{12,16},{16,20},{20,24},{24,28},{28,32},{32,36}... | collective-permute-start | bytes 98312 | tf_op jit(solution)/shard_map/ppermute | solution.py:287
  37.7 7.1 %copy-start = (s32[1,1,1,32,512]{4,3,2,1,0:T(8,128)S(1)}, s32[1,1,1,32,512]{4,3,2,1,0:T(8,128)}, u32[]{:S(2)}) copy-start(s32[1,1,1,32,512]{4,3,2,1,0:T(8,128)} %neigh_ref.3) | copy-start | bytes 196612
  37.7 7.1 %copy-start.1 = (s32[1,1,1,32,512]{4,3,2,1,0:T(8,128)S(1)}, s32[1,1,1,32,512]{4,3,2,1,0:T(8,128)}, u32[]{:S(2)}) copy-start(s32[1,1,1,32,512]{4,3,2,1,0:T(8,128)} %live_ref.3) | copy-start | bytes 196612
  37.7 7.0 %collective-permute-start.3 = (f32[3,64,128]{2,1,0:T(8,128)S(1)}, f32[3,64,128]{2,1,0:T(8,128)S(1)}, u32[]{:S(2)}, u32[]{:S(2)}) collective-permute-start(f32[3,64,128]{2,1,0:T(8,128)S(1)} %pad_maximum_fusion.1.o_ref), channel_id=1, source_target_pairs={{64,0},{128,64},{192,128},{256,192},{320,256},{384,320},{448,384},... | collective-permute-start | bytes 294920 | tf_op jit(solution)/shard_map/ppermute | solution.py:288
  41.3 3.5 %collective-permute-start.2 = (f32[3,64,128]{2,1,0:T(8,128)S(1)}, f32[3,64,128]{2,1,0:T(8,128)S(1)}, u32[]{:S(2)}, u32[]{:S(2)}) collective-permute-start(f32[3,64,128]{2,1,0:T(8,128)S(1)} %pad_maximum_fusion.1.o_ref), channel_id=1, source_target_pairs={{0,64},{64,128},{128,192},{192,256},{256,320},{320,384},{384,448},... | collective-permute-start | bytes 294920 | tf_op jit(solution)/shard_map/ppermute | solution.py:287
  52.1 22.7 %collective-permute-start.5 = (f32[96,128]{1,0:T(8,128)S(1)}, f32[96,128]{1,0:T(8,128)S(1)}, u32[]{:S(2)}, u32[]{:S(2)}) collective-permute-start(f32[96,128]{1,0:T(8,128)S(1)} %get-tuple-element.13), channel_id=1, source_target_pairs={{4,0},{8,4},{12,8},{16,12},{20,16},{24,20},{28,24},{32,28},{36,32}... | collective-permute-start | bytes 147464 | tf_op jit(solution)/shard_map/ppermute | solution.py:288
  54.0 20.8 %collective-permute-start.4 = (f32[96,128]{1,0:T(8,128)S(1)}, f32[96,128]{1,0:T(8,128)S(1)}, u32[]{:S(2)}, u32[]{:S(2)}) collective-permute-start(f32[96,128]{1,0:T(8,128)S(1)} %get-tuple-element.13), channel_id=1, source_target_pairs={{0,4},{4,8},{8,12},{12,16},{16,20},{20,24},{24,28},{28,32},{32,36}... | collective-permute-start | bytes 147464 | tf_op jit(solution)/shard_map/ppermute | solution.py:287
  74.9 16.4 %collective-permute-start.7 = (f32[3,96,128]{2,1,0:T(8,128)S(1)}, f32[3,96,128]{2,1,0:T(8,128)S(1)}, u32[]{:S(2)}, u32[]{:S(2)}) collective-permute-start(f32[3,96,128]{2,1,0:T(8,128)S(1)} %pad_maximum_fusion.fo_ref), channel_id=1, source_target_pairs={{64,0},{128,64},{192,128},{256,192},{320,256},{384,320},{448,384},... | collective-permute-start | bytes 442376 | tf_op jit(solution)/shard_map/ppermute | solution.py:288
  75.5 15.8 %collective-permute-start.6 = (f32[3,96,128]{2,1,0:T(8,128)S(1)}, f32[3,96,128]{2,1,0:T(8,128)S(1)}, u32[]{:S(2)}, u32[]{:S(2)}) collective-permute-start(f32[3,96,128]{2,1,0:T(8,128)S(1)} %pad_maximum_fusion.fo_ref), channel_id=1, source_target_pairs={{0,64},{64,128},{128,192},{192,256},{256,320},{320,384},{384,448},... | collective-permute-start | bytes 442376 | tf_op jit(solution)/shard_map/ppermute | solution.py:287

commit v3 on v2

--- a/solution.py
+++ b/solution.py
@@ -10,7 +10,8 @@
 NEIGH = 32
 TEMPLATE = 128
 GX = ("gx_0", "gx_1")
-GXZ = ("gx_0", "gx_1", "gz")
+X_Z = ("gx_0", "gz")
+CORE_Y = ("gx_1", "gy")
 COLUMN = 4
 CHUNKS = 4
 LIVE = 32
@@ -27,10 +28,12 @@
 HBM = pl.BlockSpec(memory_space=pltpu.HBM)
 
 
-def call(kernel, outs, specs, scratch=(), limit=4 << 20):
+def call(kernel, outs, specs, scratch=(), limit=4 << 20, types=None):
     return pl.pallas_call(
         kernel,
-        out_shape=[jax.ShapeDtypeStruct(shape, F32) for shape in outs],
+        out_shape=[
+            jax.ShapeDtypeStruct(shape, kind) for shape, kind in zip(outs, types or [F32] * len(outs))
+        ],
         in_specs=specs,
         out_specs=[VMEM] * len(outs),
         scratch_shapes=list(scratch),
@@ -75,7 +78,12 @@
         out_ref[copy, 32:48, :] = atoms
 
 
-def events_kernel(column_ref, map_ref, moved_ref, vel_ref, atoms_ref, low_ref, high_ref, shift_ref):
+def events_kernel(
+    column_ref, map_ref, neigh_ref, live_ref, moved_ref, vel_ref, pairs_ref,
+    atoms_ref, low_ref, high_ref, shift_ref,
+):
+    pairs_ref[0:NEIGH, :] = neigh_ref[0, 0, 0, :, :]
+    pairs_ref[NEIGH:, :] = live_ref[0, 0, 0, :, :]
     atoms_ref[...] = jnp.zeros(atoms_ref.shape, F32)
     first = jnp.int32(0)
     lane_weights = jnp.zeros((1, LANES), F32)
@@ -140,21 +148,26 @@
         moved_ref[pl.ds(48 + z * 4, 4), :] = column_ref[z, 12:16, :]
 
 
-def own_forces(z, source, neigh_ref, live_ref, table_ref):
-    for k in range(NEIGH):
-        ab, dz = divmod(k % 27, 3)
-        a, b = divmod(ab, 3)
-        first = ((z + dz + 3) & 3) * 4
-        for c in range(4):
-            for q in range(CHUNKS):
-                table_ref[c, q, k : k + 1, :] = source(a, b, c, first + q)
+def domain_forces(z, firsts, source, pairs_ref, table_ref):
+    for a in range(3):
+        for b in range(3):
+            for dz in range(3):
+                k = firsts[a][b] + dz
+                first = ((z + dz + 3) & 3) * 4
+                for c in range(4):
+                    for q in range(CHUNKS):
+                        table_ref[c, q, pl.ds(k, 1), :] = source(a, b, c, first + q)
+    for c in range(4):
+        for q in range(CHUNKS):
+            table_ref[c, q, 27:NEIGH, :] = table_ref[c, q, 0 : NEIGH - 27, :]
     forces = [[None] * CHUNKS for _ in range(3)]
     for t in range(CHUNKS):
         own = [source(1, 1, c, z * 4 + t) for c in range(4)]
         total = [jnp.zeros((8, LANES), F32)] * 3
+        cut = pl.ds(t * LANES, LANES)
         for g in range(NEIGH // 8):
-            atoms = neigh_ref[0, 0, 0, 8 * g : 8 * g + 8, t * LANES : (t + 1) * LANES]
-            live = live_ref[0, 0, 0, 8 * g : 8 * g + 8, t * LANES : (t + 1) * LANES].astype(F32)
+            atoms = pairs_ref[8 * g : 8 * g + 8, cut]
+            live = pairs_ref[NEIGH + 8 * g : NEIGH + 8 * g + 8, cut].astype(F32)
             low, high = atoms & (LANES - 1), atoms >> 7
             taken = []
             for c in range(4):
@@ -177,6 +190,12 @@
     return forces
 
 
+def directions(where_ref):
+    odd = [where_ref[n] & 1 for n in range(2)]
+    spots = [(2 - 2 * flag, 1, 2 * flag) for flag in odd]
+    return [[9 * a + 3 * b for b in spots[1]] for a in spots[0]]
+
+
 def three_sums(forces, speeds):
     pairs = ((forces, speeds), (speeds, speeds), (forces, forces))
     lane = lax.broadcasted_iota(jnp.int32, (1, LANES), 1)
@@ -206,37 +225,38 @@
     return scale * ((1.0 - mixing) * speed + ratio * force) + time_step * force
 
 
-def first_kernel(z_ref, m_ref, o_ref, p_ref, vel_ref, neigh_ref, live_ref, out_ref, table_ref):
-    z = z_ref[0]
+def first_kernel(
+    where_ref, m_ref, o_ref, p_ref, vel_ref, pairs_ref, pairs_m_ref, pairs_p_ref,
+    out_ref, sums_ref, table_ref,
+):
+    z = where_ref[2]
+    step = 1 - 2 * (z & 1)
+    firsts = directions(where_ref)
     halo = (m_ref, o_ref, p_ref)
     source = lambda a, b, c, row: halo[a][b, pl.ds(c * 16 + row, 1), :]
-    forces = own_forces(z, source, neigh_ref, live_ref, table_ref)
-    speeds = [
-        [vel_ref[pl.ds(c * 16 + z * 4 + t, 1), :] for t in range(CHUNKS)] for c in range(3)
-    ]
-    sums = three_sums(forces, speeds)
-    for copy in range(COLUMN):
+    out_ref[0:48, :] = jnp.zeros((48, LANES), F32)
+    out_ref[48:96, :] = vel_ref[...]
+    places = ((z, pairs_ref), ((z + step) & 3, pairs_m_ref), ((z - step) & 3, pairs_p_ref))
+    for place, pairs in places:
+        forces = domain_forces(place, firsts, source, pairs, table_ref)
         for c in range(3):
             for t in range(CHUNKS):
-                out_ref[copy, c * 4 + t : c * 4 + t + 1, :] = forces[c][t]
-        out_ref[copy, 12:16, :] = jnp.broadcast_to(sums, (4, LANES))
-
-
-def column_kernel(parts_ref, vel_ref, out_ref, sums_ref):
-    for z in range(COLUMN):
-        for c in range(3):
-            out_ref[pl.ds(c * 16 + z * 4, 4), :] = parts_ref[z, c * 4 : c * 4 + 4, :]
-    out_ref[48:96, :] = vel_ref[...]
-    total = sum(parts_ref[z, 12:13, :] for z in range(COLUMN))
-    for n in range(sums_ref.shape[0]):
-        sums_ref[n, :, :] = total
+                out_ref[pl.ds(c * 16 + place * 4 + t, 1), :] = forces[c][t]
+        if pairs is pairs_ref:
+            speeds = [
+                [vel_ref[pl.ds(c * 16 + z * 4 + t, 1), :] for t in range(CHUNKS)]
+                for c in range(3)
+            ]
+            sums = three_sums(forces, speeds)
+            for n in range(sums_ref.shape[0]):
+                sums_ref[n, :, :] = sums
 
 
 def second_kernel(
-    z_ref, m_ref, o_ref, p_ref, fm_ref, fo_ref, fp_ref, sums_ref, neigh_ref, live_ref,
+    where_ref, m_ref, o_ref, p_ref, fm_ref, fo_ref, fp_ref, sums_ref, pairs_ref,
     out_ref, own_sums_ref, table_ref, new_ref,
 ):
-    z = z_ref[0]
+    z = where_ref[2]
     factors = mix_factors(read_sums(jnp.sum(sums_ref[...], axis=0)))
     halo, pushed = (m_ref, o_ref, p_ref), (fm_ref, fo_ref, fp_ref)
     for a in range(3):
@@ -247,7 +267,7 @@
             if a == 1 and b == 1:
                 new_ref[9, 0:48, :] = speed
     source = lambda a, b, c, row: new_ref[a * 3 + b, pl.ds(c * 16 + row, 1), :]
-    forces = own_forces(z, source, neigh_ref, live_ref, table_ref)
+    forces = domain_forces(z, directions(where_ref), source, pairs_ref, table_ref)
     own = lambda n: [
         [new_ref[n, pl.ds(c * 16 + z * 4 + t, 1), :] for t in range(CHUNKS)] for c in range(3)
     ]
@@ -283,16 +303,20 @@
 
 def both_sides(x, axis):
     size = lax.axis_size(axis)
-    up = [(i, (i + 1) % size) for i in range(size)]
-    before = lax.ppermute(x, axis, up)
-    after = lax.ppermute(x, axis, [(j, i) for i, j in up])
-    return before, after
-
-
-def joined(before, x, after):
-    row = jnp.stack([before, x, after])
-    before, after = both_sides(row, GX)
-    return before, row, after
+    first = [(i, i ^ 1) for i in range(size)]
+    second = [(i, (i - 1 + 2 * (i % 2)) % size) for i in range(size)]
+    return lax.ppermute(x, axis, first), lax.ppermute(x, axis, second)
+
+
+def halves(x):
+    first, second = both_sides(x, "gy")
+    return first, x, second
+
+
+def joined(first, x, second):
+    row = jnp.stack([first, x, second])
+    first, second = both_sides(row, GX)
+    return first, row, second
 
 
 def shards(
@@ -306,47 +330,43 @@
     event_weight,
     template_map,
 ):
-    x_size, y_size = lax.axis_size(GX), lax.axis_size("gy")
-    z = lax.axis_index("gz").astype(jnp.int32).reshape(1)
+    half_x, size_y = lax.axis_size("gx_0"), lax.axis_size("gy")
+    where = jnp.stack([lax.axis_index(axis) for axis in ("gx_1", "gy", "gz")]).astype(jnp.int32)
     inputs = (event_count, positions, velocity, atom_eps, event_weight, event_atoms)
     staged = [pltpu.VMEM(x.shape, x.dtype) for x in inputs[1:]]
     staged += [pltpu.SemaphoreType.DMA((len(staged),))]
     (own,) = call(pack_kernel, [(COLUMN, 48, LANES)], [SMEM] + [HBM] * 5, staged, None)(*inputs)
     column = exchanged(own, "gz")
-    moved, speeds = call(
+    moved, speeds, pairs = call(
         events_kernel,
-        [(64, LANES), (48, LANES)],
-        [VMEM] * 2,
+        [(64, LANES), (48, LANES), (2 * NEIGH, CHUNKS * LANES)],
+        [VMEM] * 4,
         [
             pltpu.VMEM((LIVE + EV_DEV, LANES), F32),
             pltpu.VMEM((LIVE, LANES), jnp.int32),
             pltpu.VMEM((LIVE, LANES), jnp.int32),
             pltpu.VMEM((9, LIVE, LANES), F32),
         ],
-    )(column, template_map)
-    before, after = both_sides(moved, "gy")
-    around = joined(before, moved, after)
+        types=[F32, F32, jnp.int32],
+    )(column, template_map, neighbours, pair_live)
+    around = joined(*halves(moved))
     table = pltpu.VMEM((4, CHUNKS, NEIGH, LANES), F32)
-    (pushed,) = call(first_kernel, [(COLUMN, 16, LANES)], [SMEM] + [VMEM] * 6, [table])(
-        z, *around, speeds, neighbours, pair_live
-    )
-    pushed = exchanged(pushed, "gz")
-    forces, sums = call(column_kernel, [(96, LANES), (x_size, 1, LANES)], [VMEM] * 2)(
-        pushed, speeds
-    )
-    before, after = both_sides(forces, "gy")
-    sums = exchanged(sums, GX)
-    before, after, sums = lax.optimization_barrier((before, after, sums))
-    forces_around = joined(before, forces, after)
-    sums = exchanged(added_for_each(sums, y_size), "gy")
+    forces, sums = call(
+        first_kernel, [(96, LANES), (half_x * COLUMN, 1, LANES)], [SMEM] + [VMEM] * 7, [table]
+    )(where, *around, speeds, pairs, *both_sides(pairs, "gz"))
+    first, forces, second = halves(forces)
+    sums = exchanged(sums, X_Z)
+    first, second, sums = lax.optimization_barrier((first, second, sums))
+    forces_around = joined(first, forces, second)
+    sums = exchanged(added_for_each(sums, 2 * size_y), CORE_Y)
     result, sums = call(
         second_kernel,
-        [(40, LANES), (x_size * COLUMN, 1, LANES)],
-        [SMEM] + [VMEM] * 9,
+        [(40, LANES), (half_x * COLUMN, 1, LANES)],
+        [SMEM] + [VMEM] * 8,
         [table, pltpu.VMEM((10, 64, LANES), F32)],
-    )(z, *around, *forces_around, sums, neighbours, pair_live)
-    sums = exchanged(sums, GXZ)
-    sums = exchanged(added_for_each(sums, y_size), "gy")
+    )(where, *around, *forces_around, sums, pairs)
+    sums = exchanged(sums, X_Z)
+    sums = exchanged(added_for_each(sums, 2 * size_y), CORE_Y)
     return tuple(
         call(final_kernel, [positions.shape, velocity.shape], [VMEM] * 2)(result, sums)
     )

time: 122 us -> 132 us (1.082)
  starting transfers between devices: 31.7 us -> 45.3 us
  waiting for transfers between devices: 6.22 us -> 1.21 us
  Pallas kernels: 5.24 us -> 7.36 us
    ppermute x8 -> x10, starting transfers between devices: 31.7 us -> 45.3 us  [both_sides(): return (lax.ppermute(x, axis, first), lax.ppermute(x, axis, second))]
    ppermute x8 -> x10, waiting for transfers between devices: 6.22 us -> 1.21 us  [both_sides(): return (lax.ppermute(x, axis, first), lax.ppermute(x, axis, second))]
    pallas_call x4 -> x3, Pallas kernels: 3.05 us -> 5.14 us  [the longest x1 2.16 us: shards(): call(first_kernel, [(96, LANES), (half_x * COLUMN, 1, LANES)], [SMEM] + [...]
    all_to_all x6 -> x5, blocking collectives: 76.7 us -> 75.7 us  [exchanged(): return lax.all_to_all(x, axes, 0, 0, tiled=True)]
  transfers between devices with their start and end apart: 8 -> 10, of which waited for: 2 -> 2; matrix products, arithmetic and copies ran while one was open for 0% -> 0% of each run, Pallas kernels for 0% -> 0%
where the time goes in v3:
time: 132 us; the launch traced here: 131 us
  blocking collectives  75.7 us (57%)
  starting transfers between devices  45.3 us (34%)
  Pallas kernels  7.36 us (6%)
  between operations  1.46 us (1%)
    all_to_all x5, blocking collectives, exchanged(): return lax.all_to_all(x, axes, 0, 0, tiled=True)  75.7 us
    ppermute x10, starting transfers between devices, both_sides(): return (lax.ppermute(x, axis, first), lax.ppermute(x, axis, second))  45.3 us
  transfers between devices with their start and end apart: 10, of which 2 were waited for; matrix products, arithmetic and copies ran while one was open for 0% of the time, Pallas kernels for 0%

profile of v3, /device:TPU:1, one launch (start us, length us, event | category | flops | bytes accessed | tf_op | source)
XLA Modules:
  0.0 131.3 jit_solution(8770239137337382972)
XLA Ops:
  1.3 1.5 %shard_map.104 = f32[4,48,128]{2,1,0:T(8,128)} custom-call(s32[1,1,1]{2,1,0:T(1,128)S(6)} %copy.11.count_ref, f32[3,1,1,1,512]{4,3,2,1,0:T(1,128)} %pos_hbm.1, f32[3,1,1,1,512]{4,3,2,1,0:T(1,128)} %vel_hbm.1, f32[1,1,1,512]{3,2,1,0:T(1,128)} %eps_hbm.1, f32[1,1,1,16]{3,2,1,0:T(1,128)} %weight_hbm.1, s32[1,1,1,16,128]{4,3,2,1,0:T(8,128)} %atoms_hbm.1), custom_call_target="tpu_custom_call" | custom-call | flops 10000 | bytes 100000 | tf_op jit(solution)/shard_map/pallas_call | solution.py:338
  2.8 0.0 copy-start
  2.8 0.0 copy-start.1
  2.8 0.0 copy-start.2
  2.8 9.6 %all_to_all.25.column_ref = f32[4,48,128]{2,1,0:T(8,128)S(1)} all-to-all(f32[4,48,128]{2,1,0:T(8,128)} %shard_map.104), channel_id=1, replica_groups=mesh['gx_0'=8,'gx_1'=2,'gy'=16,'gz'=4] {'gz'}, dimensions={0} | all-to-all | bytes 196608 | tf_op jit(solution)/shard_map/all_to_all | solution.py:297
  12.4 0.0 copy-done
  12.4 0.0 copy-done.1
  12.4 0.0 copy-done.2
  12.4 1.5 %shard_map.105 = (f32[64,128]{1,0:T(8,128)S(1)}, f32[48,128]{1,0:T(8,128)S(1)}, s32[64,512]{1,0:T(8,128)S(1)}) custom-call(f32[4,48,128]{2,1,0:T(8,128)S(1)} %all_to_all.25.column_ref, f32[128,128]{1,0:T(8,128)S(1)} %copy-done, s32[1,1,1,32,512]{4,3,2,1,0:T(8,128)S(1)} %copy-done.1, s32[1,1,1,32,512]{4,3,2,1,0:T(8,128)S(1)} %copy-done.2), custom_call_target="tpu_custom_call" | custom-call | flops 10000 | bytes 100000 | tf_op jit(solution)/shard_map/pallas_call | solution.py:340
  13.9 17.9 %collective-permute-start.1 = (f32[64,128]{1,0:T(8,128)S(1)}, f32[64,128]{1,0:T(8,128)S(1)}, u32[]{:S(2)}, u32[]{:S(2)}) collective-permute-start(f32[64,128]{1,0:T(8,128)S(1)} %get-tuple-element.12), channel_id=1, source_target_pairs={{0,60},{4,8},{8,4},{12,16},{16,12},{20,24},{24,20},{28,32},{32,28}... | collective-permute-start | bytes 98312 | tf_op jit(solution)/shard_map/ppermute | solution.py:308
  31.9 1.9 %collective-permute-start = (f32[64,128]{1,0:T(8,128)S(1)}, f32[64,128]{1,0:T(8,128)S(1)}, u32[]{:S(2)}, u32[]{:S(2)}) collective-permute-start(f32[64,128]{1,0:T(8,128)S(1)} %get-tuple-element.12), channel_id=1, source_target_pairs={{0,4},{4,0},{8,12},{12,8},{16,20},{20,16},{24,28},{28,24},{32,36},... | collective-permute-start | bytes 98312 | tf_op jit(solution)/shard_map/ppermute | solution.py:308
  33.8 2.8 %collective-permute-start.5 = (s32[64,512]{1,0:T(8,128)S(1)}, s32[64,512]{1,0:T(8,128)S(1)}, u32[]{:S(2)}, u32[]{:S(2)}) collective-permute-start(s32[64,512]{1,0:T(8,128)S(1)} %get-tuple-element.14.pairs_ref), channel_id=1, source_target_pairs={{0,3},{1,2},{2,1},{3,0},{4,7},{5,6},{6,5},{7,4},{8,11},{9,10},{10,... | collective-permute-start | bytes 393224 | tf_op jit(solution)/shard_map/ppermute | solution.py:308
  36.6 1.9 %collective-permute-start.4 = (s32[64,512]{1,0:T(8,128)S(1)}, s32[64,512]{1,0:T(8,128)S(1)}, u32[]{:S(2)}, u32[]{:S(2)}) collective-permute-start(s32[64,512]{1,0:T(8,128)S(1)} %get-tuple-element.14.pairs_ref), channel_id=1, source_target_pairs={{0,1},{1,0},{2,3},{3,2},{4,5},{5,4},{6,7},{7,6},{8,9},{9,8},{10,11... | collective-permute-start | bytes 393224 | tf_op jit(solution)/shard_map/ppermute | solution.py:308
  38.5 0.0 collective-permute-done.1
  38.6 0.0 collective-permute-done
  38.6 5.8 %collective-permute-start.3 = (f32[3,64,128]{2,1,0:T(8,128)S(1)}, f32[3,64,128]{2,1,0:T(8,128)S(1)}, u32[]{:S(2)}, u32[]{:S(2)}) collective-permute-start(f32[3,64,128]{2,1,0:T(8,128)S(1)} %pad_maximum_fusion.1.o_ref), channel_id=1, source_target_pairs={{0,960},{64,128},{128,64},{192,256},{256,192},{320,384},{384,320},... | collective-permute-start | bytes 294920 | tf_op jit(solution)/shard_map/ppermute | solution.py:308
  44.3 1.9 %collective-permute-start.2 = (f32[3,64,128]{2,1,0:T(8,128)S(1)}, f32[3,64,128]{2,1,0:T(8,128)S(1)}, u32[]{:S(2)}, u32[]{:S(2)}) collective-permute-start(f32[3,64,128]{2,1,0:T(8,128)S(1)} %pad_maximum_fusion.1.o_ref), channel_id=1, source_target_pairs={{0,64},{64,0},{128,192},{192,128},{256,320},{320,256},{384,448},{4... | collective-permute-start | bytes 294920 | tf_op jit(solution)/shard_map/ppermute | solution.py:308
  46.3 0.1 pad_add_fusion.where_ref
  46.4 0.3 collective-permute-done.3.p_ref
  46.6 0.9 collective-permute-done.2.m_ref
  47.5 0.0 collective-permute-done.5.pairs_p_ref
  47.5 0.0 collective-permute-done.4.pairs_m_ref
  47.5 2.2 %shard_map.106 = (f32[96,128]{1,0:T(8,128)S(1)}, f32[32,1,128]{2,1,0:T(1,128)S(1)}) custom-call(s32[3]{0:T(128)S(1)} %pad_add_fusion.where_ref, f32[3,64,128]{2,1,0:T(8,128)S(1)} %collective-permute-done.2.m_ref, f32[3,64,128]{2,1,0:T(8,128)S(1)} %pad_maximum_fusion.1.o_ref, f32[3,64,128]{2,1,0:T(8,128)S(1)} %collective-permute-done.3.p_ref, ...), custom_call_target="tpu_custom_call" | custom-call | flops 10000 | bytes 100000 | tf_op jit(solution)/shard_map/pallas_call | solution.py:354
  49.7 2.7 %collective-permute-start.7 = (f32[96,128]{1,0:T(8,128)S(1)}, f32[96,128]{1,0:T(8,128)S(1)}, u32[]{:S(2)}, u32[]{:S(2)}) collective-permute-start(f32[96,128]{1,0:T(8,128)S(1)} %get-tuple-element.15), channel_id=1, source_target_pairs={{0,60},{4,8},{8,4},{12,16},{16,12},{20,24},{24,20},{28,32},{32,28}... | collective-permute-start | bytes 147464 | tf_op jit(solution)/shard_map/ppermute | solution.py:308
  52.4 2.8 %collective-permute-start.6 = (f32[96,128]{1,0:T(8,128)S(1)}, f32[96,128]{1,0:T(8,128)S(1)}, u32[]{:S(2)}, u32[]{:S(2)}) collective-permute-start(f32[96,128]{1,0:T(8,128)S(1)} %get-tuple-element.15), channel_id=1, source_target_pairs={{0,4},{4,0},{8,12},{12,8},{16,20},{20,16},{24,28},{28,24},{32,36},... | collective-permute-start | bytes 147464 | tf_op jit(solution)/shard_map/ppermute | solution.py:308
  55.3 17.7 %all_to_all.26 = f32[32,1,128]{2,1,0:T(1,128)S(1)} all-to-all(f32[32,1,128]{2,1,0:T(1,128)S(1)} %get-tuple-element.16), channel_id=1, replica_groups=mesh['gx_0'=8,'gx_1'=2,'gy'=16,'gz'=4] {'gx_0','gz'}, dimensions={0} | all-to-all | bytes 32768 | tf_op jit(solution)/shard_map/all_to_all | solution.py:297
  73.0 0.0 collective-permute-done.7
  73.0 0.0 collective-permute-done.6
  73.0 5.6 %collective-permute-start.9 = (f32[3,96,128]{2,1,0:T(8,128)S(1)}, f32[3,96,128]{2,1,0:T(8,128)S(1)}, u32[]{:S(2)}, u32[]{:S(2)}) collective-permute-start(f32[3,96,128]{2,1,0:T(8,128)S(1)} %pad_maximum_fusion.fo_ref), channel_id=1, source_target_pairs={{0,960},{64,128},{128,64},{192,256},{256,192},{320,384},{384,320},... | collective-permute-start | bytes 442376 | tf_op jit(solution)/shard_map/ppermute | solution.py:308
  78.6 1.9 %collective-permute-start.8 = (f32[3,96,128]{2,1,0:T(8,128)S(1)}, f32[3,96,128]{2,1,0:T(8,128)S(1)}, u32[]{:S(2)}, u32[]{:S(2)}) collective-permute-start(f32[3,96,128]{2,1,0:T(8,128)S(1)} %pad_maximum_fusion.fo_ref), channel_id=1, source_target_pairs={{0,64},{64,0},{128,192},{192,128},{256,320},{320,256},{384,448},{4... | collective-permute-start | bytes 442376 | tf_op jit(solution)/shard_map/ppermute | solution.py:308
  80.5 0.1 reduce_sum.18
  80.6 18.7 %all_to_all.27.sums_ref = f32[32,1,128]{2,1,0:T(1,128)S(1)} all-to-all(f32[32,1,128]{2,1,0:T(1,128)S(1)} %broadcast_in_dim.4), channel_id=1, replica_groups=mesh['gx_0'=8,'gx_1'=2,'gy'=16,'gz'=4] {'gx_1','gy'}, dimensions={0} | all-to-all | bytes 32768 | tf_op jit(solution)/shard_map/all_to_all | solution.py:297
  99.3 0.0 collective-permute-done.9.fp_ref
  99.3 0.0 collective-permute-done.8.fm_ref
  99.3 1.5 %shard_map.107 = (f32[40,128]{1,0:T(8,128)S(1)}, f32[32,1,128]{2,1,0:T(1,128)S(1)}) custom-call(s32[3]{0:T(128)S(1)} %pad_add_fusion.where_ref, f32[3,64,128]{2,1,0:T(8,128)S(1)} %collective-permute-done.2.m_ref, f32[3,64,128]{2,1,0:T(8,128)S(1)} %pad_maximum_fusion.1.o_ref, f32[3,64,128]{2,1,0:T(8,128)S(1)} %collective-permute-done.3.p_ref, ...), custom_call_target="tpu_custom_call" | custom-call | flops 10000 | bytes 100000 | tf_op jit(solution)/shard_map/pallas_call | solution.py:362
  100.8 13.1 %all_to_all.28 = f32[32,1,128]{2,1,0:T(1,128)S(1)} all-to-all(f32[32,1,128]{2,1,0:T(1,128)S(1)} %get-tuple-element.21), channel_id=1, replica_groups=mesh['gx_0'=8,'gx_1'=2,'gy'=16,'gz'=4] {'gx_0','gz'}, dimensions={0} | all-to-all | bytes 32768 | tf_op jit(solution)/shard_map/all_to_all | solution.py:297
  113.9 0.1 reduce_sum.19
  114.0 16.5 %all_to_all.29.sums_ref = f32[32,1,128]{2,1,0:T(1,128)S(1)} all-to-all(f32[32,1,128]{2,1,0:T(1,128)S(1)} %broadcast_in_dim.5), channel_id=1, replica_groups=mesh['gx_0'=8,'gx_1'=2,'gy'=16,'gz'=4] {'gx_1','gy'}, dimensions={0} | all-to-all | bytes 32768 | tf_op jit(solution)/shard_map/all_to_all | solution.py:297
  130.5 0.7 shard_map.108
  (4 shorter events, 0.0 us)
Async XLA Ops:
  2.8 9.7 %copy-start = (f32[128,128]{1,0:T(8,128)S(1)}, f32[128,128]{1,0:T(8,128)}, u32[]{:S(2)}) copy-start(f32[128,128]{1,0:T(8,128)} %map_ref.1) | copy-start | bytes 196612
  2.8 9.7 %copy-start.1 = (s32[1,1,1,32,512]{4,3,2,1,0:T(8,128)S(1)}, s32[1,1,1,32,512]{4,3,2,1,0:T(8,128)}, u32[]{:S(2)}) copy-start(s32[1,1,1,32,512]{4,3,2,1,0:T(8,128)} %neigh_ref.1) | copy-start | bytes 196612
  2.8 9.6 %copy-start.2 = (s32[1,1,1,32,512]{4,3,2,1,0:T(8,128)S(1)}, s32[1,1,1,32,512]{4,3,2,1,0:T(8,128)}, u32[]{:S(2)}) copy-start(s32[1,1,1,32,512]{4,3,2,1,0:T(8,128)} %live_ref.1) | copy-start | bytes 196612
  13.9 24.6 %collective-permute-start.1 = (f32[64,128]{1,0:T(8,128)S(1)}, f32[64,128]{1,0:T(8,128)S(1)}, u32[]{:S(2)}, u32[]{:S(2)}) collective-permute-start(f32[64,128]{1,0:T(8,128)S(1)} %get-tuple-element.12), channel_id=1, source_target_pairs={{0,60},{4,8},{8,4},{12,16},{16,12},{20,24},{24,20},{28,32},{32,28}... | collective-permute-start | bytes 98312 | tf_op jit(solution)/shard_map/ppermute | solution.py:308
  31.9 6.7 %collective-permute-start = (f32[64,128]{1,0:T(8,128)S(1)}, f32[64,128]{1,0:T(8,128)S(1)}, u32[]{:S(2)}, u32[]{:S(2)}) collective-permute-start(f32[64,128]{1,0:T(8,128)S(1)} %get-tuple-element.12), channel_id=1, source_target_pairs={{0,4},{4,0},{8,12},{12,8},{16,20},{20,16},{24,28},{28,24},{32,36},... | collective-permute-start | bytes 98312 | tf_op jit(solution)/shard_map/ppermute | solution.py:308
  33.8 13.7 %collective-permute-start.5 = (s32[64,512]{1,0:T(8,128)S(1)}, s32[64,512]{1,0:T(8,128)S(1)}, u32[]{:S(2)}, u32[]{:S(2)}) collective-permute-start(s32[64,512]{1,0:T(8,128)S(1)} %get-tuple-element.14.pairs_ref), channel_id=1, source_target_pairs={{0,3},{1,2},{2,1},{3,0},{4,7},{5,6},{6,5},{7,4},{8,11},{9,10},{10,... | collective-permute-start | bytes 393224 | tf_op jit(solution)/shard_map/ppermute | solution.py:308
  36.6 10.9 %collective-permute-start.4 = (s32[64,512]{1,0:T(8,128)S(1)}, s32[64,512]{1,0:T(8,128)S(1)}, u32[]{:S(2)}, u32[]{:S(2)}) collective-permute-start(s32[64,512]{1,0:T(8,128)S(1)} %get-tuple-element.14.pairs_ref), channel_id=1, source_target_pairs={{0,1},{1,0},{2,3},{3,2},{4,5},{5,4},{6,7},{7,6},{8,9},{9,8},{10,11... | collective-permute-start | bytes 393224 | tf_op jit(solution)/shard_map/ppermute | solution.py:308
  38.6 8.0 %collective-permute-start.3 = (f32[3,64,128]{2,1,0:T(8,128)S(1)}, f32[3,64,128]{2,1,0:T(8,128)S(1)}, u32[]{:S(2)}, u32[]{:S(2)}) collective-permute-start(f32[3,64,128]{2,1,0:T(8,128)S(1)} %pad_maximum_fusion.1.o_ref), channel_id=1, source_target_pairs={{0,960},{64,128},{128,64},{192,256},{256,192},{320,384},{384,320},... | collective-permute-start | bytes 294920 | tf_op jit(solution)/shard_map/ppermute | solution.py:308
  44.3 3.2 %collective-permute-start.2 = (f32[3,64,128]{2,1,0:T(8,128)S(1)}, f32[3,64,128]{2,1,0:T(8,128)S(1)}, u32[]{:S(2)}, u32[]{:S(2)}) collective-permute-start(f32[3,64,128]{2,1,0:T(8,128)S(1)} %pad_maximum_fusion.1.o_ref), channel_id=1, source_target_pairs={{0,64},{64,0},{128,192},{192,128},{256,320},{320,256},{384,448},{4... | collective-permute-start | bytes 294920 | tf_op jit(solution)/shard_map/ppermute | solution.py:308
  49.7 23.3 %collective-permute-start.7 = (f32[96,128]{1,0:T(8,128)S(1)}, f32[96,128]{1,0:T(8,128)S(1)}, u32[]{:S(2)}, u32[]{:S(2)}) collective-permute-start(f32[96,128]{1,0:T(8,128)S(1)} %get-tuple-element.15), channel_id=1, source_target_pairs={{0,60},{4,8},{8,4},{12,16},{16,12},{20,24},{24,20},{28,32},{32,28}... | collective-permute-start | bytes 147464 | tf_op jit(solution)/shard_map/ppermute | solution.py:308
  52.4 20.5 %collective-permute-start.6 = (f32[96,128]{1,0:T(8,128)S(1)}, f32[96,128]{1,0:T(8,128)S(1)}, u32[]{:S(2)}, u32[]{:S(2)}) collective-permute-start(f32[96,128]{1,0:T(8,128)S(1)} %get-tuple-element.15), channel_id=1, source_target_pairs={{0,4},{4,0},{8,12},{12,8},{16,20},{20,16},{24,28},{28,24},{32,36},... | collective-permute-start | bytes 147464 | tf_op jit(solution)/shard_map/ppermute | solution.py:308
  73.0 26.3 %collective-permute-start.9 = (f32[3,96,128]{2,1,0:T(8,128)S(1)}, f32[3,96,128]{2,1,0:T(8,128)S(1)}, u32[]{:S(2)}, u32[]{:S(2)}) collective-permute-start(f32[3,96,128]{2,1,0:T(8,128)S(1)} %pad_maximum_fusion.fo_ref), channel_id=1, source_target_pairs={{0,960},{64,128},{128,64},{192,256},{256,192},{320,384},{384,320},... | collective-permute-start | bytes 442376 | tf_op jit(solution)/shard_map/ppermute | solution.py:308
  78.6 20.7 %collective-permute-start.8 = (f32[3,96,128]{2,1,0:T(8,128)S(1)}, f32[3,96,128]{2,1,0:T(8,128)S(1)}, u32[]{:S(2)}, u32[]{:S(2)}) collective-permute-start(f32[3,96,128]{2,1,0:T(8,128)S(1)} %pad_maximum_fusion.fo_ref), channel_id=1, source_target_pairs={{0,64},{64,0},{128,192},{192,128},{256,320},{320,256},{384,448},{4... | collective-permute-start | bytes 442376 | tf_op jit(solution)/shard_map/ppermute | solution.py:308

commit v4 on v2

--- a/solution.py
+++ b/solution.py
@@ -5,6 +5,7 @@
 from jax.experimental.pallas import tpu as pltpu
 from jax.sharding import Mesh
 from jax.sharding import PartitionSpec as P
+
 
 EV_DEV = 16
 NEIGH = 32
@@ -331,14 +332,14 @@
         z, *around, speeds, neighbours, pair_live
     )
     pushed = exchanged(pushed, "gz")
-    forces, sums = call(column_kernel, [(96, LANES), (x_size, 1, LANES)], [VMEM] * 2)(
+    forces, sums = call(column_kernel, [(96, LANES), (y_size, 1, LANES)], [VMEM] * 2)(
         pushed, speeds
     )
+    sums = exchanged(sums, "gy")
     before, after = both_sides(forces, "gy")
-    sums = exchanged(sums, GX)
     before, after, sums = lax.optimization_barrier((before, after, sums))
     forces_around = joined(before, forces, after)
-    sums = exchanged(added_for_each(sums, y_size), "gy")
+    sums = exchanged(added_for_each(sums, x_size), GX)
     result, sums = call(
         second_kernel,
         [(40, LANES), (x_size * COLUMN, 1, LANES)],

time: 122 us -> 121 us (level)
  blocking collectives: 76.7 us -> 72.1 us
  starting transfers between devices: 31.7 us -> 35.2 us
    ppermute x4, starting transfers between devices: 24.1 us -> 28.7 us  [both_sides(): after = lax.ppermute(x, axis, [(j, i) for i, j in up])]
    all_to_all x6, blocking collectives: 76.7 us -> 72.1 us  [exchanged(): return lax.all_to_all(x, axes, 0, 0, tiled=True)]
where the time goes in v4:
time: 121 us; the launch traced here: 120 us
  blocking collectives  72.1 us (60%)
  starting transfers between devices  35.2 us (29%)
  waiting for transfers between devices  6.22 us (5%)
  Pallas kernels  5.24 us (4%)
  between operations  1.38 us (1%)
    all_to_all x6, blocking collectives, exchanged(): return lax.all_to_all(x, axes, 0, 0, tiled=True)  72.1 us
    ppermute x4, starting transfers between devices, both_sides(): after = lax.ppermute(x, axis, [(j, i) for i, j in up])  28.7 us
    ppermute x4, starting transfers between devices, both_sides(): before = lax.ppermute(x, axis, up)  6.49 us
    ppermute x4, waiting for transfers between devices, both_sides(): before = lax.ppermute(x, axis, up)  3.94 us
  transfers between devices with their start and end apart: 8, of which 2 were waited for; matrix products, arithmetic and copies ran while one was open for 0% of the time, Pallas kernels for 0%

profile of v4, /device:TPU:1, one launch (start us, length us, event | category | flops | bytes accessed | tf_op | source)
XLA Modules:
  0.0 120.3 jit_solution(11863995839603274083)
XLA Ops:
  1.3 1.5 %shard_map.104 = f32[4,48,128]{2,1,0:T(8,128)} custom-call(s32[1,1,1]{2,1,0:T(1,128)S(6)} %copy.11.count_ref, f32[3,1,1,1,512]{4,3,2,1,0:T(1,128)} %pos_hbm.1, f32[3,1,1,1,512]{4,3,2,1,0:T(1,128)} %vel_hbm.1, f32[1,1,1,512]{3,2,1,0:T(1,128)} %eps_hbm.1, f32[1,1,1,16]{3,2,1,0:T(1,128)} %weight_hbm.1, s32[1,1,1,16,128]{4,3,2,1,0:T(8,128)} %atoms_hbm.1), custom_call_target="tpu_custom_call" | custom-call | flops 10000 | bytes 100000 | tf_op jit(solution)/shard_map/pallas_call | solution.py:315
  2.8 0.0 copy-start.2
  2.8 9.6 %all_to_all.30.column_ref = f32[4,48,128]{2,1,0:T(8,128)S(1)} all-to-all(f32[4,48,128]{2,1,0:T(8,128)} %shard_map.104), channel_id=1, replica_groups=mesh['gx_0'=8,'gx_1'=2,'gy'=16,'gz'=4] {'gz'}, dimensions={0} | all-to-all | bytes 196608 | tf_op jit(solution)/shard_map/all_to_all | solution.py:278
  12.4 0.0 copy-done.2
  12.4 1.5 %shard_map.105 = (f32[64,128]{1,0:T(8,128)S(1)}, f32[48,128]{1,0:T(8,128)S(1)}) custom-call(f32[4,48,128]{2,1,0:T(8,128)S(1)} %all_to_all.30.column_ref, f32[128,128]{1,0:T(8,128)S(1)} %copy-done.2), custom_call_target="tpu_custom_call" | custom-call | flops 10000 | bytes 100000 | tf_op jit(solution)/shard_map/pallas_call | solution.py:317
  13.9 17.9 %collective-permute-start.1 = (f32[64,128]{1,0:T(8,128)S(1)}, f32[64,128]{1,0:T(8,128)S(1)}, u32[]{:S(2)}, u32[]{:S(2)}) collective-permute-start(f32[64,128]{1,0:T(8,128)S(1)} %get-tuple-element.11), channel_id=1, source_target_pairs={{4,0},{8,4},{12,8},{16,12},{20,16},{24,20},{28,24},{32,28},{36,32}... | collective-permute-start | bytes 98312 | tf_op jit(solution)/shard_map/ppermute | solution.py:289
  31.8 1.9 %collective-permute-start = (f32[64,128]{1,0:T(8,128)S(1)}, f32[64,128]{1,0:T(8,128)S(1)}, u32[]{:S(2)}, u32[]{:S(2)}) collective-permute-start(f32[64,128]{1,0:T(8,128)S(1)} %get-tuple-element.11), channel_id=1, source_target_pairs={{0,4},{4,8},{8,12},{12,16},{16,20},{20,24},{24,28},{28,32},{32,36}... | collective-permute-start | bytes 98312 | tf_op jit(solution)/shard_map/ppermute | solution.py:288
  33.8 0.0 collective-permute-done.1
  33.8 3.9 %collective-permute-done = f32[64,128]{1,0:T(8,128)S(1)} collective-permute-done((f32[64,128]{1,0:T(8,128)S(1)}, f32[64,128]{1,0:T(8,128)S(1)}, u32[]{:S(2)}, u32[]{:S(2)}) %collective-permute-start) | collective-permute-done | bytes 32800 | tf_op jit(solution)/shard_map/ppermute | solution.py:288
  37.7 0.0 copy-start
  37.7 0.0 copy-start.1
  37.7 3.5 %collective-permute-start.3 = (f32[3,64,128]{2,1,0:T(8,128)S(1)}, f32[3,64,128]{2,1,0:T(8,128)S(1)}, u32[]{:S(2)}, u32[]{:S(2)}) collective-permute-start(f32[3,64,128]{2,1,0:T(8,128)S(1)} %pad_maximum_fusion.1.o_ref), channel_id=1, source_target_pairs={{64,0},{128,64},{192,128},{256,192},{320,256},{384,320},{448,384},... | collective-permute-start | bytes 294920 | tf_op jit(solution)/shard_map/ppermute | solution.py:289
  41.3 1.2 %collective-permute-start.2 = (f32[3,64,128]{2,1,0:T(8,128)S(1)}, f32[3,64,128]{2,1,0:T(8,128)S(1)}, u32[]{:S(2)}, u32[]{:S(2)}) collective-permute-start(f32[3,64,128]{2,1,0:T(8,128)S(1)} %pad_maximum_fusion.1.o_ref), channel_id=1, source_target_pairs={{0,64},{64,128},{128,192},{192,256},{256,320},{320,384},{384,448},... | collective-permute-start | bytes 294920 | tf_op jit(solution)/shard_map/ppermute | solution.py:288
  42.5 2.3 %collective-permute-done.3.p_ref = f32[3,64,128]{2,1,0:T(8,128)S(1)} collective-permute-done((f32[3,64,128]{2,1,0:T(8,128)S(1)}, f32[3,64,128]{2,1,0:T(8,128)S(1)}, u32[]{:S(2)}, u32[]{:S(2)}) %collective-permute-start.3) | collective-permute-done | bytes 98336 | tf_op jit(solution)/shard_map/ppermute | solution.py:289
  44.8 0.0 collective-permute-done.2.m_ref
  44.8 0.0 copy-done
  44.8 0.0 copy-done.1
  44.8 0.7 shard_map.106
  45.4 6.6 %all_to_all.31.parts_ref = f32[4,16,128]{2,1,0:T(8,128)S(1)} all-to-all(f32[4,16,128]{2,1,0:T(8,128)S(1)} %shard_map.106), channel_id=1, replica_groups=mesh['gx_0'=8,'gx_1'=2,'gy'=16,'gz'=4] {'gz'}, dimensions={0} | all-to-all | bytes 65536 | tf_op jit(solution)/shard_map/all_to_all | solution.py:278
  52.1 1.9 %collective-permute-start.5 = (f32[96,128]{1,0:T(8,128)S(1)}, f32[96,128]{1,0:T(8,128)S(1)}, u32[]{:S(2)}, u32[]{:S(2)}) collective-permute-start(f32[96,128]{1,0:T(8,128)S(1)} %get-tuple-element.13), channel_id=1, source_target_pairs={{4,0},{8,4},{12,8},{16,12},{20,16},{24,20},{28,24},{32,28},{36,32}... | collective-permute-start | bytes 147464 | tf_op jit(solution)/shard_map/ppermute | solution.py:289
  54.0 3.4 %collective-permute-start.4 = (f32[96,128]{1,0:T(8,128)S(1)}, f32[96,128]{1,0:T(8,128)S(1)}, u32[]{:S(2)}, u32[]{:S(2)}) collective-permute-start(f32[96,128]{1,0:T(8,128)S(1)} %get-tuple-element.13), channel_id=1, source_target_pairs={{0,4},{4,8},{8,12},{12,16},{16,20},{20,24},{24,28},{28,32},{32,36}... | collective-permute-start | bytes 147464 | tf_op jit(solution)/shard_map/ppermute | solution.py:288
  57.4 14.9 %all_to_all.32 = f32[16,1,128]{2,1,0:T(1,128)S(1)} all-to-all(f32[16,1,128]{2,1,0:T(1,128)S(1)} %get-tuple-element.14), channel_id=1, replica_groups=mesh['gx_0'=8,'gx_1'=2,'gy'=16,'gz'=4] {'gy'}, dimensions={0} | all-to-all | bytes 16384 | tf_op jit(solution)/shard_map/all_to_all | solution.py:278
  72.3 0.0 collective-permute-done.5
  72.3 0.0 collective-permute-done.4
  72.3 5.3 %collective-permute-start.7 = (f32[3,96,128]{2,1,0:T(8,128)S(1)}, f32[3,96,128]{2,1,0:T(8,128)S(1)}, u32[]{:S(2)}, u32[]{:S(2)}) collective-permute-start(f32[3,96,128]{2,1,0:T(8,128)S(1)} %pad_maximum_fusion.fo_ref), channel_id=1, source_target_pairs={{64,0},{128,64},{192,128},{256,192},{320,256},{384,320},{448,384},... | collective-permute-start | bytes 442376 | tf_op jit(solution)/shard_map/ppermute | solution.py:289
  77.6 0.0 collective-permute-start.6
  77.6 13.9 %all_to_all.33.sums_ref = f32[16,1,128]{2,1,0:T(1,128)S(1)} all-to-all(f32[16,1,128]{2,1,0:T(1,128)S(1)} %broadcast_in_dim.4), channel_id=1, replica_groups=mesh['gx_0'=8,'gx_1'=2,'gy'=16,'gz'=4] {'gx_0','gx_1'}, dimensions={0} | all-to-all | bytes 16384 | tf_op jit(solution)/shard_map/all_to_all | solution.py:278
  91.5 0.0 collective-permute-done.7.fp_ref
  91.5 0.0 collective-permute-done.6.fm_ref
  91.5 0.9 shard_map.108
  92.4 13.2 %all_to_all.34 = f32[64,1,128]{2,1,0:T(1,128)S(1)} all-to-all(f32[64,1,128]{2,1,0:T(1,128)S(1)} %get-tuple-element.19), channel_id=1, replica_groups=mesh['gx_0'=8,'gx_1'=2,'gy'=16,'gz'=4] {'gx_0','gx_1','gz'}, dimensions={0} | all-to-all | bytes 65536 | tf_op jit(solution)/shard_map/all_to_all | solution.py:278
  105.6 0.1 reduce_sum.19
  105.7 13.8 %all_to_all.35.sums_ref = f32[16,1,128]{2,1,0:T(1,128)S(1)} all-to-all(f32[16,1,128]{2,1,0:T(1,128)S(1)} %broadcast_in_dim.5), channel_id=1, replica_groups=mesh['gx_0'=8,'gx_1'=2,'gy'=16,'gz'=4] {'gy'}, dimensions={0} | all-to-all | bytes 16384 | tf_op jit(solution)/shard_map/all_to_all | solution.py:278
  119.5 0.7 shard_map.109
  (6 shorter events, 0.1 us)
Async XLA Ops:
  2.8 9.6 %copy-start.2 = (f32[128,128]{1,0:T(8,128)S(1)}, f32[128,128]{1,0:T(8,128)}, u32[]{:S(2)}) copy-start(f32[128,128]{1,0:T(8,128)} %map_ref.1) | copy-start | bytes 196612
  13.9 19.9 %collective-permute-start.1 = (f32[64,128]{1,0:T(8,128)S(1)}, f32[64,128]{1,0:T(8,128)S(1)}, u32[]{:S(2)}, u32[]{:S(2)}) collective-permute-start(f32[64,128]{1,0:T(8,128)S(1)} %get-tuple-element.11), channel_id=1, source_target_pairs={{4,0},{8,4},{12,8},{16,12},{20,16},{24,20},{28,24},{32,28},{36,32}... | collective-permute-start | bytes 98312 | tf_op jit(solution)/shard_map/ppermute | solution.py:289
  31.8 5.9 %collective-permute-start = (f32[64,128]{1,0:T(8,128)S(1)}, f32[64,128]{1,0:T(8,128)S(1)}, u32[]{:S(2)}, u32[]{:S(2)}) collective-permute-start(f32[64,128]{1,0:T(8,128)S(1)} %get-tuple-element.11), channel_id=1, source_target_pairs={{0,4},{4,8},{8,12},{12,16},{16,20},{20,24},{24,28},{28,32},{32,36}... | collective-permute-start | bytes 98312 | tf_op jit(solution)/shard_map/ppermute | solution.py:288
  37.7 7.1 %copy-start = (s32[1,1,1,32,512]{4,3,2,1,0:T(8,128)S(1)}, s32[1,1,1,32,512]{4,3,2,1,0:T(8,128)}, u32[]{:S(2)}) copy-start(s32[1,1,1,32,512]{4,3,2,1,0:T(8,128)} %neigh_ref.3) | copy-start | bytes 196612
  37.7 7.1 %copy-start.1 = (s32[1,1,1,32,512]{4,3,2,1,0:T(8,128)S(1)}, s32[1,1,1,32,512]{4,3,2,1,0:T(8,128)}, u32[]{:S(2)}) copy-start(s32[1,1,1,32,512]{4,3,2,1,0:T(8,128)} %live_ref.3) | copy-start | bytes 196612
  37.7 7.0 %collective-permute-start.3 = (f32[3,64,128]{2,1,0:T(8,128)S(1)}, f32[3,64,128]{2,1,0:T(8,128)S(1)}, u32[]{:S(2)}, u32[]{:S(2)}) collective-permute-start(f32[3,64,128]{2,1,0:T(8,128)S(1)} %pad_maximum_fusion.1.o_ref), channel_id=1, source_target_pairs={{64,0},{128,64},{192,128},{256,192},{320,256},{384,320},{448,384},... | collective-permute-start | bytes 294920 | tf_op jit(solution)/shard_map/ppermute | solution.py:289
  41.3 3.5 %collective-permute-start.2 = (f32[3,64,128]{2,1,0:T(8,128)S(1)}, f32[3,64,128]{2,1,0:T(8,128)S(1)}, u32[]{:S(2)}, u32[]{:S(2)}) collective-permute-start(f32[3,64,128]{2,1,0:T(8,128)S(1)} %pad_maximum_fusion.1.o_ref), channel_id=1, source_target_pairs={{0,64},{64,128},{128,192},{192,256},{256,320},{320,384},{384,448},... | collective-permute-start | bytes 294920 | tf_op jit(solution)/shard_map/ppermute | solution.py:288
  52.1 20.2 %collective-permute-start.5 = (f32[96,128]{1,0:T(8,128)S(1)}, f32[96,128]{1,0:T(8,128)S(1)}, u32[]{:S(2)}, u32[]{:S(2)}) collective-permute-start(f32[96,128]{1,0:T(8,128)S(1)} %get-tuple-element.13), channel_id=1, source_target_pairs={{4,0},{8,4},{12,8},{16,12},{20,16},{24,20},{28,24},{32,28},{36,32}... | collective-permute-start | bytes 147464 | tf_op jit(solution)/shard_map/ppermute | solution.py:289
  54.0 18.3 %collective-permute-start.4 = (f32[96,128]{1,0:T(8,128)S(1)}, f32[96,128]{1,0:T(8,128)S(1)}, u32[]{:S(2)}, u32[]{:S(2)}) collective-permute-start(f32[96,128]{1,0:T(8,128)S(1)} %get-tuple-element.13), channel_id=1, source_target_pairs={{0,4},{4,8},{8,12},{12,16},{16,20},{20,24},{24,28},{28,32},{32,36}... | collective-permute-start | bytes 147464 | tf_op jit(solution)/shard_map/ppermute | solution.py:288
  72.3 19.2 %collective-permute-start.7 = (f32[3,96,128]{2,1,0:T(8,128)S(1)}, f32[3,96,128]{2,1,0:T(8,128)S(1)}, u32[]{:S(2)}, u32[]{:S(2)}) collective-permute-start(f32[3,96,128]{2,1,0:T(8,128)S(1)} %pad_maximum_fusion.fo_ref), channel_id=1, source_target_pairs={{64,0},{128,64},{192,128},{256,192},{320,256},{384,320},{448,384},... | collective-permute-start | bytes 442376 | tf_op jit(solution)/shard_map/ppermute | solution.py:289
  77.6 13.9 %collective-permute-start.6 = (f32[3,96,128]{2,1,0:T(8,128)S(1)}, f32[3,96,128]{2,1,0:T(8,128)S(1)}, u32[]{:S(2)}, u32[]{:S(2)}) collective-permute-start(f32[3,96,128]{2,1,0:T(8,128)S(1)} %pad_maximum_fusion.fo_ref), channel_id=1, source_target_pairs={{0,64},{64,128},{128,192},{192,256},{256,320},{320,384},{384,448},... | collective-permute-start | bytes 442376 | tf_op jit(solution)/shard_map/ppermute | solution.py:288

commit v5 on v4

--- a/solution.py
+++ b/solution.py
@@ -12,6 +12,8 @@
 TEMPLATE = 128
 GX = ("gx_0", "gx_1")
 GXZ = ("gx_0", "gx_1", "gz")
+X_Y = ("gx_0", "gy")
+CORE_Z = ("gx_1", "gz")
 COLUMN = 4
 CHUNKS = 4
 LIVE = 32
@@ -216,19 +218,20 @@
         [vel_ref[pl.ds(c * 16 + z * 4 + t, 1), :] for t in range(CHUNKS)] for c in range(3)
     ]
     sums = three_sums(forces, speeds)
-    for copy in range(COLUMN):
+    for copy in range(out_ref.shape[0]):
         for c in range(3):
             for t in range(CHUNKS):
                 out_ref[copy, c * 4 + t : c * 4 + t + 1, :] = forces[c][t]
         out_ref[copy, 12:16, :] = jnp.broadcast_to(sums, (4, LANES))
 
 
-def column_kernel(parts_ref, vel_ref, out_ref, sums_ref):
+def column_kernel(where_ref, parts_ref, vel_ref, out_ref, sums_ref):
+    first = where_ref[1] * COLUMN
     for z in range(COLUMN):
         for c in range(3):
-            out_ref[pl.ds(c * 16 + z * 4, 4), :] = parts_ref[z, c * 4 : c * 4 + 4, :]
+            out_ref[pl.ds(c * 16 + z * 4, 4), :] = parts_ref[first + z, c * 4 : c * 4 + 4, :]
     out_ref[48:96, :] = vel_ref[...]
-    total = sum(parts_ref[z, 12:13, :] for z in range(COLUMN))
+    total = sum(parts_ref[n, 12:13, :] for n in range(parts_ref.shape[0]))
     for n in range(sums_ref.shape[0]):
         sums_ref[n, :, :] = total
 
@@ -308,7 +311,7 @@
     template_map,
 ):
     x_size, y_size = lax.axis_size(GX), lax.axis_size("gy")
-    z = lax.axis_index("gz").astype(jnp.int32).reshape(1)
+    z = jnp.stack([lax.axis_index("gz"), lax.axis_index("gx_1")]).astype(jnp.int32)
     inputs = (event_count, positions, velocity, atom_eps, event_weight, event_atoms)
     staged = [pltpu.VMEM(x.shape, x.dtype) for x in inputs[1:]]
     staged += [pltpu.SemaphoreType.DMA((len(staged),))]
@@ -328,18 +331,16 @@
     before, after = both_sides(moved, "gy")
     around = joined(before, moved, after)
     table = pltpu.VMEM((4, CHUNKS, NEIGH, LANES), F32)
-    (pushed,) = call(first_kernel, [(COLUMN, 16, LANES)], [SMEM] + [VMEM] * 6, [table])(
+    (pushed,) = call(first_kernel, [(2 * COLUMN, 16, LANES)], [SMEM] + [VMEM] * 6, [table])(
         z, *around, speeds, neighbours, pair_live
     )
-    pushed = exchanged(pushed, "gz")
-    forces, sums = call(column_kernel, [(96, LANES), (y_size, 1, LANES)], [VMEM] * 2)(
-        pushed, speeds
-    )
-    sums = exchanged(sums, "gy")
+    pushed = exchanged(pushed, CORE_Z)
+    forces, sums = call(
+        column_kernel, [(96, LANES), (x_size // 2 * y_size, 1, LANES)], [SMEM] + [VMEM] * 2
+    )(z, pushed, speeds)
     before, after = both_sides(forces, "gy")
-    before, after, sums = lax.optimization_barrier((before, after, sums))
+    sums = exchanged(sums, X_Y)
     forces_around = joined(before, forces, after)
-    sums = exchanged(added_for_each(sums, x_size), GX)
     result, sums = call(
         second_kernel,
         [(40, LANES), (x_size * COLUMN, 1, LANES)],

time: 121 us -> 122 us (level)
  blocking collectives: 72.1 us -> 50.7 us
  waiting for transfers between devices: 6.22 us -> 19.3 us
  starting transfers between devices: 35.2 us -> 42.2 us
  Pallas kernels: 5.24 us -> 7.62 us
    all_to_all x6 -> x4, blocking collectives: 72.1 us -> 50.7 us  [exchanged(): return lax.all_to_all(x, axes, 0, 0, tiled=True)]
    all_to_all x0 -> x1, starting transfers between devices: none -> 10.6 us  [exchanged(): return lax.all_to_all(x, axes, 0, 0, tiled=True)]
    all_to_all x0 -> x1, waiting for transfers between devices: none -> 9.76 us  [exchanged(): return lax.all_to_all(x, axes, 0, 0, tiled=True)]
    ppermute x4, starting transfers between devices: 28.7 us -> 24.4 us  [both_sides(): after = lax.ppermute(x, axis, [(j, i) for i, j in up])]
    ppermute x4, waiting for transfers between devices: 2.28 us -> 5.62 us  [both_sides(): after = lax.ppermute(x, axis, [(j, i) for i, j in up])]
    pallas_call x2, Pallas kernels: 0.67 us -> 2.4 us  [the longest x1 1.21 us: shards(): call(column_kernel, [(96, LANES), (x_size // 2 * y_size, 1, LANES)], [SME...]
  transfers between devices with their start and end apart: 8 -> 9, of which waited for: 2 -> 4; matrix products, arithmetic and copies ran while one was open for 0% -> 0% of each run, Pallas kernels for 0% -> 0%
where the time goes in v5:
time: 122 us; the launch traced here: 121 us
  blocking collectives  50.7 us (42%)
  starting transfers between devices  42.2 us (35%)
  waiting for transfers between devices  19.3 us (16%)
  Pallas kernels  7.62 us (6%)
  between operations  1.4 us (1%)
    all_to_all x4, blocking collectives, exchanged(): return lax.all_to_all(x, axes, 0, 0, tiled=True)  50.7 us
    ppermute x4, starting transfers between devices, both_sides(): after = lax.ppermute(x, axis, [(j, i) for i, j in up])  24.4 us
    all_to_all x1, starting transfers between devices, exchanged(): return lax.all_to_all(x, axes, 0, 0, tiled=True)  10.6 us
    all_to_all x1, waiting for transfers between devices, exchanged(): return lax.all_to_all(x, axes, 0, 0, tiled=True)  9.76 us
    ppermute x4, starting transfers between devices, both_sides(): before = lax.ppermute(x, axis, up)  7.28 us
    ppermute x4, waiting for transfers between devices, both_sides(): after = lax.ppermute(x, axis, [(j, i) for i, j in up])  5.62 us
    ppermute x4, waiting for transfers between devices, both_sides(): before = lax.ppermute(x, axis, up)  3.93 us
  transfers between devices with their start and end apart: 9, of which 4 were waited for; matrix products, arithmetic and copies ran while one was open for 0% of the time, Pallas kernels for 0%

profile of v5, /device:TPU:1, one launch (start us, length us, event | category | flops | bytes accessed | tf_op | source)
XLA Modules:
  0.0 121.4 jit_solution(18289292983627231248)
XLA Ops:
  1.3 1.5 %shard_map.104 = f32[4,48,128]{2,1,0:T(8,128)} custom-call(s32[1,1,1]{2,1,0:T(1,128)S(6)} %copy.11.count_ref, f32[3,1,1,1,512]{4,3,2,1,0:T(1,128)} %pos_hbm.1, f32[3,1,1,1,512]{4,3,2,1,0:T(1,128)} %vel_hbm.1, f32[1,1,1,512]{3,2,1,0:T(1,128)} %eps_hbm.1, f32[1,1,1,16]{3,2,1,0:T(1,128)} %weight_hbm.1, s32[1,1,1,16,128]{4,3,2,1,0:T(8,128)} %atoms_hbm.1), custom_call_target="tpu_custom_call" | custom-call | flops 10000 | bytes 100000 | tf_op jit(solution)/shard_map/pallas_call | solution.py:318
  2.7 0.0 copy-start.2
  2.8 9.6 %all_to_all.25.column_ref = f32[4,48,128]{2,1,0:T(8,128)S(1)} all-to-all(f32[4,48,128]{2,1,0:T(8,128)} %shard_map.104), channel_id=1, replica_groups=mesh['gx_0'=8,'gx_1'=2,'gy'=16,'gz'=4] {'gz'}, dimensions={0} | all-to-all | bytes 196608 | tf_op jit(solution)/shard_map/all_to_all | solution.py:281
  12.4 0.0 copy-done.2
  12.4 1.5 %shard_map.105 = (f32[64,128]{1,0:T(8,128)S(1)}, f32[48,128]{1,0:T(8,128)S(1)}) custom-call(f32[4,48,128]{2,1,0:T(8,128)S(1)} %all_to_all.25.column_ref, f32[128,128]{1,0:T(8,128)S(1)} %copy-done.2), custom_call_target="tpu_custom_call" | custom-call | flops 10000 | bytes 100000 | tf_op jit(solution)/shard_map/pallas_call | solution.py:320
  13.9 17.9 %collective-permute-start.1 = (f32[64,128]{1,0:T(8,128)S(1)}, f32[64,128]{1,0:T(8,128)S(1)}, u32[]{:S(2)}, u32[]{:S(2)}) collective-permute-start(f32[64,128]{1,0:T(8,128)S(1)} %get-tuple-element.8), channel_id=1, source_target_pairs={{4,0},{8,4},{12,8},{16,12},{20,16},{24,20},{28,24},{32,28},{36,32}... | collective-permute-start | bytes 98312 | tf_op jit(solution)/shard_map/ppermute | solution.py:292
  31.8 1.9 %collective-permute-start = (f32[64,128]{1,0:T(8,128)S(1)}, f32[64,128]{1,0:T(8,128)S(1)}, u32[]{:S(2)}, u32[]{:S(2)}) collective-permute-start(f32[64,128]{1,0:T(8,128)S(1)} %get-tuple-element.8), channel_id=1, source_target_pairs={{0,4},{4,8},{8,12},{12,16},{16,20},{20,24},{24,28},{28,32},{32,36}... | collective-permute-start | bytes 98312 | tf_op jit(solution)/shard_map/ppermute | solution.py:291
  33.8 0.0 collective-permute-done.1
  33.8 3.9 %collective-permute-done = f32[64,128]{1,0:T(8,128)S(1)} collective-permute-done((f32[64,128]{1,0:T(8,128)S(1)}, f32[64,128]{1,0:T(8,128)S(1)}, u32[]{:S(2)}, u32[]{:S(2)}) %collective-permute-start) | collective-permute-done | bytes 32800 | tf_op jit(solution)/shard_map/ppermute | solution.py:291
  37.7 0.0 copy-start
  37.7 0.0 copy-start.1
  37.7 3.5 %collective-permute-start.3 = (f32[3,64,128]{2,1,0:T(8,128)S(1)}, f32[3,64,128]{2,1,0:T(8,128)S(1)}, u32[]{:S(2)}, u32[]{:S(2)}) collective-permute-start(f32[3,64,128]{2,1,0:T(8,128)S(1)} %pad_maximum_fusion.1.o_ref), channel_id=1, source_target_pairs={{64,0},{128,64},{192,128},{256,192},{320,256},{384,320},{448,384},... | collective-permute-start | bytes 294920 | tf_op jit(solution)/shard_map/ppermute | solution.py:292
  41.3 1.2 collective-permute-start.2
  42.5 0.1 pad_add_fusion.z_ref.where_ref
  42.5 2.2 %collective-permute-done.3.p_ref = f32[3,64,128]{2,1,0:T(8,128)S(1)} collective-permute-done((f32[3,64,128]{2,1,0:T(8,128)S(1)}, f32[3,64,128]{2,1,0:T(8,128)S(1)}, u32[]{:S(2)}, u32[]{:S(2)}) %collective-permute-start.3) | collective-permute-done | bytes 98336 | tf_op jit(solution)/shard_map/ppermute | solution.py:292
  44.7 0.0 collective-permute-done.2.m_ref
  44.7 0.0 copy-done
  44.7 0.0 copy-done.1
  44.8 1.2 shard_map.106
  46.0 9.7 %all_to_all.26.parts_ref = f32[8,16,128]{2,1,0:T(8,128)S(1)} all-to-all(f32[8,16,128]{2,1,0:T(8,128)S(1)} %shard_map.106), channel_id=1, replica_groups=mesh['gx_0'=8,'gx_1'=2,'gy'=16,'gz'=4] {'gx_1','gz'}, dimensions={0} | all-to-all | bytes 131072 | tf_op jit(solution)/shard_map/all_to_all | solution.py:281
  55.7 1.2 shard_map.107
  56.9 1.9 %collective-permute-start.5 = (f32[96,128]{1,0:T(8,128)S(1)}, f32[96,128]{1,0:T(8,128)S(1)}, u32[]{:S(2)}, u32[]{:S(2)}) collective-permute-start(f32[96,128]{1,0:T(8,128)S(1)} %get-tuple-element.10), channel_id=1, source_target_pairs={{4,0},{8,4},{12,8},{16,12},{20,16},{24,20},{28,24},{32,28},{36,32}... | collective-permute-start | bytes 147464 | tf_op jit(solution)/shard_map/ppermute | solution.py:292
  58.8 3.4 %collective-permute-start.4 = (f32[96,128]{1,0:T(8,128)S(1)}, f32[96,128]{1,0:T(8,128)S(1)}, u32[]{:S(2)}, u32[]{:S(2)}) collective-permute-start(f32[96,128]{1,0:T(8,128)S(1)} %get-tuple-element.10), channel_id=1, source_target_pairs={{0,4},{4,8},{8,12},{12,16},{16,20},{20,24},{24,28},{28,32},{32,36}... | collective-permute-start | bytes 147464 | tf_op jit(solution)/shard_map/ppermute | solution.py:291
  62.2 10.6 %all-to-all-start.2 = ((f32[128,1,128]{2,1,0:T(1,128)}), f32[128,1,128]{2,1,0:T(1,128)S(1)}, u32[]{:S(2)}, u32[]{:S(2)}) async-start(f32[128,1,128]{2,1,0:T(1,128)} %get-tuple-element.11), calls=%async_computation.2 | async-start | bytes 131072 | tf_op jit(solution)/shard_map/all_to_all | solution.py:281
  72.7 0.0 collective-permute-done.5
  72.8 0.0 collective-permute-done.4
  72.8 1.0 collective-permute-start.7
  73.7 0.8 collective-permute-start.6
  74.5 3.4 %collective-permute-done.7.fp_ref = f32[3,96,128]{2,1,0:T(8,128)S(1)} collective-permute-done((f32[3,96,128]{2,1,0:T(8,128)S(1)}, f32[3,96,128]{2,1,0:T(8,128)S(1)}, u32[]{:S(2)}, u32[]{:S(2)}) %collective-permute-start.7) | collective-permute-done | bytes 147488 | tf_op jit(solution)/shard_map/ppermute | solution.py:292
  78.0 0.0 collective-permute-done.6.fm_ref
  78.0 9.8 %all-to-all-done.2.sums_ref = f32[128,1,128]{2,1,0:T(1,128)S(1)} async-done(((f32[128,1,128]{2,1,0:T(1,128)}), f32[128,1,128]{2,1,0:T(1,128)S(1)}, u32[]{:S(2)}, u32[]{:S(2)}) %all-to-all-start.2) | async-done | bytes 65568 | tf_op jit(solution)/shard_map/all_to_all | solution.py:281
  87.7 1.5 %shard_map.108 = (f32[40,128]{1,0:T(8,128)S(1)}, f32[64,1,128]{2,1,0:T(1,128)S(1)}) custom-call(s32[2]{0:T(128)S(1)} %pad_add_fusion.z_ref.where_ref, f32[3,64,128]{2,1,0:T(8,128)S(1)} %collective-permute-done.2.m_ref, f32[3,64,128]{2,1,0:T(8,128)S(1)} %pad_maximum_fusion.1.o_ref, f32[3,64,128]{2,1,0:T(8,128)S(1)} %collective-permute-done.3.p_ref, ...), custom_call_target="tpu_custom_call" | custom-call | flops 10000 | bytes 100000 | tf_op jit(solution)/shard_map/pallas_call | solution.py:344
  89.3 15.4 %all_to_all.27 = f32[64,1,128]{2,1,0:T(1,128)S(1)} all-to-all(f32[64,1,128]{2,1,0:T(1,128)S(1)} %get-tuple-element.13), channel_id=1, replica_groups=mesh['gx_0'=8,'gx_1'=2,'gy'=16,'gz'=4] {'gx_0','gx_1','gz'}, dimensions={0} | all-to-all | bytes 65536 | tf_op jit(solution)/shard_map/all_to_all | solution.py:281
  104.7 0.1 reduce_sum.9
  104.8 15.9 %all_to_all.28.sums_ref = f32[16,1,128]{2,1,0:T(1,128)S(1)} all-to-all(f32[16,1,128]{2,1,0:T(1,128)S(1)} %broadcast_in_dim.2), channel_id=1, replica_groups=mesh['gx_0'=8,'gx_1'=2,'gy'=16,'gz'=4] {'gy'}, dimensions={0} | all-to-all | bytes 16384 | tf_op jit(solution)/shard_map/all_to_all | solution.py:281
  120.7 0.7 shard_map.109
  (3 shorter events, 0.0 us)
Async XLA Ops:
  2.7 9.6 %copy-start.2 = (f32[128,128]{1,0:T(8,128)S(1)}, f32[128,128]{1,0:T(8,128)}, u32[]{:S(2)}) copy-start(f32[128,128]{1,0:T(8,128)} %map_ref.1) | copy-start | bytes 196612
  13.9 19.9 %collective-permute-start.1 = (f32[64,128]{1,0:T(8,128)S(1)}, f32[64,128]{1,0:T(8,128)S(1)}, u32[]{:S(2)}, u32[]{:S(2)}) collective-permute-start(f32[64,128]{1,0:T(8,128)S(1)} %get-tuple-element.8), channel_id=1, source_target_pairs={{4,0},{8,4},{12,8},{16,12},{20,16},{24,20},{28,24},{32,28},{36,32}... | collective-permute-start | bytes 98312 | tf_op jit(solution)/shard_map/ppermute | solution.py:292
  31.8 5.9 %collective-permute-start = (f32[64,128]{1,0:T(8,128)S(1)}, f32[64,128]{1,0:T(8,128)S(1)}, u32[]{:S(2)}, u32[]{:S(2)}) collective-permute-start(f32[64,128]{1,0:T(8,128)S(1)} %get-tuple-element.8), channel_id=1, source_target_pairs={{0,4},{4,8},{8,12},{12,16},{16,20},{20,24},{24,28},{28,32},{32,36}... | collective-permute-start | bytes 98312 | tf_op jit(solution)/shard_map/ppermute | solution.py:291
  37.7 7.1 %copy-start = (s32[1,1,1,32,512]{4,3,2,1,0:T(8,128)S(1)}, s32[1,1,1,32,512]{4,3,2,1,0:T(8,128)}, u32[]{:S(2)}) copy-start(s32[1,1,1,32,512]{4,3,2,1,0:T(8,128)} %neigh_ref.3) | copy-start | bytes 196612
  37.7 7.1 %copy-start.1 = (s32[1,1,1,32,512]{4,3,2,1,0:T(8,128)S(1)}, s32[1,1,1,32,512]{4,3,2,1,0:T(8,128)}, u32[]{:S(2)}) copy-start(s32[1,1,1,32,512]{4,3,2,1,0:T(8,128)} %live_ref.3) | copy-start | bytes 196612
  37.7 7.0 %collective-permute-start.3 = (f32[3,64,128]{2,1,0:T(8,128)S(1)}, f32[3,64,128]{2,1,0:T(8,128)S(1)}, u32[]{:S(2)}, u32[]{:S(2)}) collective-permute-start(f32[3,64,128]{2,1,0:T(8,128)S(1)} %pad_maximum_fusion.1.o_ref), channel_id=1, source_target_pairs={{64,0},{128,64},{192,128},{256,192},{320,256},{384,320},{448,384},... | collective-permute-start | bytes 294920 | tf_op jit(solution)/shard_map/ppermute | solution.py:292
  41.3 3.5 %collective-permute-start.2 = (f32[3,64,128]{2,1,0:T(8,128)S(1)}, f32[3,64,128]{2,1,0:T(8,128)S(1)}, u32[]{:S(2)}, u32[]{:S(2)}) collective-permute-start(f32[3,64,128]{2,1,0:T(8,128)S(1)} %pad_maximum_fusion.1.o_ref), channel_id=1, source_target_pairs={{0,64},{64,128},{128,192},{192,256},{256,320},{320,384},{384,448},... | collective-permute-start | bytes 294920 | tf_op jit(solution)/shard_map/ppermute | solution.py:291
  56.9 15.9 %collective-permute-start.5 = (f32[96,128]{1,0:T(8,128)S(1)}, f32[96,128]{1,0:T(8,128)S(1)}, u32[]{:S(2)}, u32[]{:S(2)}) collective-permute-start(f32[96,128]{1,0:T(8,128)S(1)} %get-tuple-element.10), channel_id=1, source_target_pairs={{4,0},{8,4},{12,8},{16,12},{20,16},{24,20},{28,24},{32,28},{36,32}... | collective-permute-start | bytes 147464 | tf_op jit(solution)/shard_map/ppermute | solution.py:292
  58.8 14.0 %collective-permute-start.4 = (f32[96,128]{1,0:T(8,128)S(1)}, f32[96,128]{1,0:T(8,128)S(1)}, u32[]{:S(2)}, u32[]{:S(2)}) collective-permute-start(f32[96,128]{1,0:T(8,128)S(1)} %get-tuple-element.10), channel_id=1, source_target_pairs={{0,4},{4,8},{8,12},{12,16},{16,20},{20,24},{24,28},{28,32},{32,36}... | collective-permute-start | bytes 147464 | tf_op jit(solution)/shard_map/ppermute | solution.py:291
  62.2 25.6 %all-to-all-start.2 = ((f32[128,1,128]{2,1,0:T(1,128)}), f32[128,1,128]{2,1,0:T(1,128)S(1)}, u32[]{:S(2)}, u32[]{:S(2)}) async-start(f32[128,1,128]{2,1,0:T(1,128)} %get-tuple-element.11), calls=%async_computation.2 | async-start | bytes 131072 | tf_op jit(solution)/shard_map/all_to_all | solution.py:281
  72.8 5.2 %collective-permute-start.7 = (f32[3,96,128]{2,1,0:T(8,128)S(1)}, f32[3,96,128]{2,1,0:T(8,128)S(1)}, u32[]{:S(2)}, u32[]{:S(2)}) collective-permute-start(f32[3,96,128]{2,1,0:T(8,128)S(1)} %pad_maximum_fusion.fo_ref), channel_id=1, source_target_pairs={{64,0},{128,64},{192,128},{256,192},{320,256},{384,320},{448,384},... | collective-permute-start | bytes 442376 | tf_op jit(solution)/shard_map/ppermute | solution.py:292
  73.7 4.2 %collective-permute-start.6 = (f32[3,96,128]{2,1,0:T(8,128)S(1)}, f32[3,96,128]{2,1,0:T(8,128)S(1)}, u32[]{:S(2)}, u32[]{:S(2)}) collective-permute-start(f32[3,96,128]{2,1,0:T(8,128)S(1)} %pad_maximum_fusion.fo_ref), channel_id=1, source_target_pairs={{0,64},{64,128},{128,192},{192,256},{256,320},{320,384},{384,448},... | collective-permute-start | bytes 442376 | tf_op jit(solution)/shard_map/ppermute | solution.py:291
